TPU v7x, 32 devices: a whole 2x2x4 slice. The times are simulated.
32 devices in a mesh: grp: 4 (over x, core), dev: 8 (over z, y).
Axes of the slice: x: 2, y: 2, z: 4, core: 2. Of those that a mesh axis runs over, the one named last changes fastest.
Arguments:
- node_features: float32 [16384, 768], P(('grp', 'dev')), may hold values from -6 to 6
- tiles: bfloat16 [896, 128, 128], P(('grp', 'dev')), may hold values from -0.1875 to 0.1875
- tile_list: int32 [896, 2], replicated, may hold values from 0 to 127, as said below
- weight: float32 [768, 768], replicated, may hold values from -0.21875 to 0.21875
- texts: float32 [1024, 768], P(('grp', 'dev')), may hold values from -6 to 6
- selected: int32 [1024], P(('grp', 'dev')), may hold values from 0 to 16383, as said below
- pairing: int32 [1024], P(('grp', 'dev')), may hold values from 0 to 1023, each once
Outputs:
- contrast_loss: float32 [], replicated
- grad_nodes: float32 [16384, 768], P(('grp', 'dev'))
- grad_weight: float32 [768, 768], replicated
- grad_texts: float32 [1024, 768], P(('grp', 'dev'))
Inputs may be any that keep to these rules, and one draw needn't show every extreme that they name: `tile_list`: device number p = grp index * (devices along dev) + dev index holds node blocks p * 4 to (p + 1) * 4 - 1 and tiles p * 28 to (p + 1) * 28 - 1. A tile's row block lies on the device that holds the tile; its column block lies on that device, on another device of the same grp index, or on the device of the same dev index in another grp. At most 2 tiles of one device have column blocks on any one other device; in every draw each device has one other device of its grp index and one of its dev index at that most. `selected`: distinct ids; the ids listed on a device are nodes of that device.
All inputs are finite; a program needn't handle non-finite values.
Results may differ from a plain program's by a relative error of at most 0.0004.
The roundings to bfloat16 on the way count: a program that leaves them out, or rounds other values in their place, can miss the bound.
Values may be sent and summed in bfloat16 or wider, within the bound.
No kernel may reach another device: no remote copies, remote signals or barrier semaphores. Data moves between devices by JAX's collectives and lax.ppermute only.
A program may use at most 128 MiB of HBM per device.

v0:
```python
import jax
import jax.numpy as jnp
from jax import lax
from jax.sharding import PartitionSpec as P

CAP = 2


SCALE = 1.0 / 0.07
EPS = 1e-06
PRECISE = lax.Precision.HIGHEST
ROOT_HALF = 0.7071067811865476
INV_ROOT_TWO_PI = 0.3989422804014327


def gelu_value(value):
    return 0.5 * value * (1.0 + lax.erf(value * ROOT_HALF))


def gelu_slope(value):
    return (
        0.5 * (1.0 + lax.erf(value * ROOT_HALF))
        + value * jnp.exp(-0.5 * value * value) * INV_ROOT_TWO_PI
    )


def slot_plan(peer_lists, peer_ids, device, blocks_dev, capacity):
    col_owner = peer_lists[:, :, 1] // blocks_dev
    wanted = (col_owner == device) & (peer_ids[:, None] != device)
    slot_order = jnp.cumsum(wanted.astype(jnp.int32), axis=1) - 1
    local_block = peer_lists[:, :, 1] - device * blocks_dev
    slot_hits = wanted[:, :, None] & (
        slot_order[:, :, None] == jnp.arange(capacity, dtype=jnp.int32)[None, None, :]
    )
    block_index = jnp.sum(jnp.where(slot_hits, local_block[:, :, None], 0), axis=1)
    slot_valid = jnp.any(slot_hits, axis=1)
    return (block_index.reshape(-1), slot_valid.reshape(-1))


def slot_pick(slot_of_tile, keep, slots_all):
    return (slot_of_tile[None, :] == jnp.arange(slots_all, dtype=jnp.int32)[:, None]) & keep[
        None, :
    ]


def land_blocks(total, block_index, valid, incoming):
    return total.at[block_index].add(jnp.where(valid[:, None, None], incoming, 0.0))


def shards(node_features, tiles, tile_list, weight, texts, selected, pairing):
    groups = lax.axis_size("grp")
    members = lax.axis_size("dev")
    grp_index = lax.axis_index("grp")
    dev_index = lax.axis_index("dev")
    device = grp_index * members + dev_index
    block_rows = tiles.shape[1]
    feat_width = node_features.shape[1]
    blocks_dev = node_features.shape[0] // block_rows
    tile_dev = tiles.shape[0]
    sel_dev = selected.shape[0]
    capacity = CAP
    total_sel = sel_dev * groups * members
    rounded = node_features.astype(jnp.bfloat16).reshape(blocks_dev, block_rows, feat_width)
    my_list = lax.dynamic_slice_in_dim(tile_list, device * tile_dev, tile_dev, 0)
    row_block = my_list[:, 0] - device * blocks_dev
    col_owner = my_list[:, 1] // blocks_dev
    col_block = my_list[:, 1] - col_owner * blocks_dev
    owner_grp = col_owner // members
    owner_dev = col_owner % members
    is_local = col_owner == device
    is_near = (owner_grp == grp_index) & jnp.logical_not(is_local)
    is_far = (owner_dev == dev_index) & (owner_grp != grp_index)
    positions = jnp.arange(tile_dev, dtype=jnp.int32)
    earlier = (col_owner[:, None] == col_owner[None, :]) & (positions[None, :] < positions[:, None])
    slot_rank = jnp.sum(earlier.astype(jnp.int32), axis=1)
    near_slot = owner_dev * capacity + slot_rank
    far_slot = owner_grp * capacity + slot_rank
    group_lists = lax.dynamic_slice_in_dim(
        tile_list, grp_index * members * tile_dev, members * tile_dev, 0
    ).reshape(members, tile_dev, 2)
    near_peers = grp_index * members + jnp.arange(members, dtype=jnp.int32)
    near_index, near_valid = slot_plan(group_lists, near_peers, device, blocks_dev, capacity)
    far_lists = lax.dynamic_index_in_dim(
        tile_list.reshape(groups, members, tile_dev, 2), dev_index, 1, False
    )
    far_peers = jnp.arange(groups, dtype=jnp.int32) * members + dev_index
    far_index, far_valid = slot_plan(far_lists, far_peers, device, blocks_dev, capacity)
    zero_half = jnp.zeros((), jnp.bfloat16)
    sel_local = selected - device * blocks_dev * block_rows
    sel_block = sel_local // block_rows
    sel_offset = sel_local % block_rows
    picked = jnp.take(tiles, sel_offset, axis=1)
    tile_rows = jnp.where((row_block[:, None] == sel_block[None, :])[:, :, None], picked, zero_half)
    near_pick = slot_pick(near_slot, is_near, members * capacity)
    far_pick = slot_pick(far_slot, is_far, groups * capacity)
    near_rows = jnp.einsum(
        "st,tkc->skc", near_pick.astype(jnp.bfloat16), tile_rows, preferred_element_type=jnp.float32
    ).astype(jnp.bfloat16)
    far_rows = jnp.einsum(
        "st,tkc->skc", far_pick.astype(jnp.bfloat16), tile_rows, preferred_element_type=jnp.float32
    ).astype(jnp.bfloat16)
    local_tile_rows = jnp.where(is_local[:, None, None], tile_rows, zero_half)
    near_send = jnp.where(
        near_valid[:, None, None], jnp.take(rounded, near_index, axis=0), zero_half
    )
    near_blocks = lax.all_to_all(
        near_send.reshape(members, capacity, block_rows, feat_width),
        "dev",
        split_axis=0,
        concat_axis=0,
        tiled=True,
    )
    far_send = jnp.where(far_valid[:, None, None], jnp.take(rounded, far_index, axis=0), zero_half)
    far_blocks = lax.all_to_all(
        far_send.reshape(groups, capacity, block_rows, feat_width),
        "grp",
        split_axis=0,
        concat_axis=0,
        tiled=True,
    )
    source_table = jnp.concatenate(
        [
            rounded,
            near_blocks.reshape(-1, block_rows, feat_width),
            far_blocks.reshape(-1, block_rows, feat_width),
        ],
        axis=0,
    )
    source_index = jnp.where(
        is_local,
        col_block,
        jnp.where(is_near, blocks_dev + near_slot, blocks_dev + members * capacity + far_slot),
    )
    sources = jnp.take(source_table, source_index, axis=0)
    messages = jnp.einsum("tkc,tcd->kd", tile_rows, sources, preferred_element_type=jnp.float32)
    chosen = node_features[sel_local] + messages
    before = jnp.dot(chosen, weight, precision=PRECISE)
    hidden = gelu_value(before)
    node_norm = jnp.sqrt(jnp.sum(hidden * hidden, axis=1, keepdims=True) + EPS)
    unit_nodes = hidden / node_norm
    text_norm = jnp.sqrt(jnp.sum(texts * texts, axis=1, keepdims=True) + EPS)
    unit_texts = texts / text_norm
    node_rows, pair_rows = (
        lax.all_gather(unit_nodes, "dev", axis=0, tiled=True),
        lax.all_gather(pairing, "dev", axis=0, tiled=True),
    )
    text_cols = lax.all_gather(unit_texts, "grp", axis=0, tiled=True)
    scores = SCALE * lax.dot_general(
        node_rows, text_cols, (((1,), (1,)), ((), ())), precision=PRECISE
    )
    exp_scores = jnp.exp(scores)
    row_total = lax.psum(jnp.sum(exp_scores, axis=1), "dev")
    col_total = lax.psum(jnp.sum(exp_scores, axis=0), "grp")
    col_global = (
        (jnp.arange(groups, dtype=jnp.int32)[:, None] * members + dev_index) * sel_dev
        + jnp.arange(sel_dev, dtype=jnp.int32)[None, :]
    ).reshape(-1)
    target = pair_rows[:, None] == col_global[None, :]
    score_grads = 0.5 * (
        exp_scores / row_total[:, None] + exp_scores / col_total[None, :]
    ) - target.astype(jnp.float32)
    node_part = SCALE * jnp.dot(score_grads, text_cols, precision=PRECISE)
    node_dir = lax.psum_scatter(node_part, "dev", scatter_dimension=0, tiled=True)
    text_part = SCALE * lax.dot_general(
        score_grads, node_rows, (((0,), (0,)), ((), ())), precision=PRECISE
    )
    text_dir = lax.psum_scatter(text_part, "grp", scatter_dimension=0, tiled=True)
    own_rows = lax.dynamic_slice_in_dim(row_total, dev_index * sel_dev, sel_dev, 0)
    own_cols = lax.dynamic_slice_in_dim(col_total, grp_index * sel_dev, sel_dev, 0)
    positive = jnp.sum(jnp.where(target, scores, 0.0))
    lse_sum, pos_sum = lax.psum(
        (jnp.sum(jnp.log(own_rows)) + jnp.sum(jnp.log(own_cols)), positive), ("grp", "dev")
    )
    contrast_loss = lse_sum / (2.0 * total_sel) - pos_sum / total_sel
    node_back = (
        node_dir - unit_nodes * jnp.sum(unit_nodes * node_dir, axis=1, keepdims=True)
    ) / node_norm
    grad_texts = (
        text_dir - unit_texts * jnp.sum(unit_texts * text_dir, axis=1, keepdims=True)
    ) / text_norm
    pre_grad = node_back * gelu_slope(before)
    weight_term = lax.dot_general(chosen, pre_grad, (((0,), (0,)), ((), ())), precision=PRECISE)
    grad_weight = lax.psum(weight_term, ("grp", "dev"))
    row_grads = lax.dot_general(pre_grad, weight, (((1,), (1,)), ((), ())), precision=PRECISE)
    rounded_grads = row_grads.astype(jnp.bfloat16)
    empty_blocks = jnp.zeros((blocks_dev, block_rows, feat_width), jnp.float32)
    local_spread = jnp.einsum(
        "tkc,kd->tcd", local_tile_rows, rounded_grads, preferred_element_type=jnp.float32
    )
    grad_blocks = empty_blocks.at[col_block].add(local_spread)
    near_rows_in = lax.all_to_all(
        near_rows.reshape(members, capacity, sel_dev, block_rows),
        "dev",
        split_axis=0,
        concat_axis=0,
        tiled=True,
    )
    near_grads_in = lax.all_gather(rounded_grads, "dev", axis=0, tiled=True).reshape(
        members, sel_dev, feat_width
    )
    near_spread = jnp.einsum(
        "pqkc,pkd->pqcd", near_rows_in, near_grads_in, preferred_element_type=jnp.float32
    )
    grad_blocks = land_blocks(
        grad_blocks, near_index, near_valid, near_spread.reshape(-1, block_rows, feat_width)
    )
    far_rows_in = lax.all_to_all(
        far_rows.reshape(groups, capacity, sel_dev, block_rows),
        "grp",
        split_axis=0,
        concat_axis=0,
        tiled=True,
    )
    far_grads_in = lax.all_gather(rounded_grads, "grp", axis=0, tiled=True).reshape(
        groups, sel_dev, feat_width
    )
    far_spread = jnp.einsum(
        "pqkc,pkd->pqcd", far_rows_in, far_grads_in, preferred_element_type=jnp.float32
    )
    grad_blocks = land_blocks(
        grad_blocks, far_index, far_valid, far_spread.reshape(-1, block_rows, feat_width)
    )
    grad_nodes = grad_blocks.reshape(-1, feat_width).at[sel_local].add(row_grads)
    return (contrast_loss, grad_nodes, grad_weight, grad_texts)


def solution(mesh):
    return jax.shard_map(
        shards,
        mesh=mesh,
        in_specs=(
            P(("grp", "dev"), None),
            P(("grp", "dev"), None, None),
            P(),
            P(),
            P(("grp", "dev"), None),
            P(("grp", "dev")),
            P(("grp", "dev")),
        ),
        out_specs=(P(), P(("grp", "dev"), None), P(), P(("grp", "dev"), None)),
        check_vma=False,
    )
```

profile of v0, /device:TPU:0, one launch (start us, length us, event | category | flops | bytes accessed | tf_op | source)
XLA Modules:
  0.0 442.9 jit_solution(16403538620831499144)
XLA Ops:
  12.5 2.8 select_select_fusion.1
  15.3 4.4 all-to-all-start.1
  21.1 2.5 gather_fusion.2
  23.9 4.0 select_select_fusion
  27.9 12.5 %all-to-all-done.1 = bf16[4,2,128,768]{3,2,1,0:T(8,128)(2,1)} async-done(((bf16[4,2,128,768]{3,2,1,0:T(8,128)(2,1)}), bf16[4,2,128,768]{3,2,1,0:T(8,128)(2,1)}, u32[]{:S(2)}, u32[]{:S(2)}) %all-to-all-start.1) | async-done | bytes 1572896 | tf_op jit(solution)/shard_map/all_to_all | solution.py:114
  40.4 6.6 %all-to-all-start = ((bf16[8,2,128,768]{3,2,1,0:T(8,128)(2,1)}), bf16[8,2,128,768]{3,2,1,0:T(8,128)(2,1)}, u32[]{:S(2)}, u32[]{:S(2)}) async-start(bf16[8,2,128,768]{3,2,1,0:T(8,128)(2,1)} %select_select_fusion), calls=%async_computation | async-start | bytes 6291456 | tf_op jit(solution)/shard_map/all_to_all | solution.py:106
  50.7 2.8 gather_fusion.1
  53.7 64.1 %all-reduce = s32[256]{0:T(256)S(1)} all-reduce(s32[256]{0:T(256)S(1)} %dynamic-update-slice), channel_id=1, replica_groups=mesh['grp'=4,'dev'=8] {'dev'}, use_global_device_ids=true, to_apply=%add | all-reduce | flops 256 | bytes 2048
  119.0 6.6 %all_gather.16 = f32[128,768]{1,0:T(8,128)} all-gather(f32[32,768]{1,0:T(8,128)S(1)} %broadcast_divide_fusion), channel_id=1, replica_groups=mesh['grp'=4,'dev'=8] {'grp'}, dimensions={0}, use_global_device_ids=true | all-gather | bytes 491520 | tf_op jit(solution)/shard_map/all_gather | solution.py:147
  126.8 5.8 %pad_maximum_fusion = bf16[28,128,768]{2,1,0:T(8,128)(2,1)} fusion(bf16[8,128,768]{2,1,0:T(8,128)(2,1)} %bitcast.17, bf16[16,128,768]{2,1,0:T(8,128)(2,1)} %bitcast.11, bf16[4,128,768]{2,1,0:T(8,128)(2,1)S(1)} %bitcast.101), kind=kLoop, calls=%fused_computation.10 | loop fusion | flops 5505024 | bytes 11010048 | tf_op jit(solution)/shard_map/concatenate | solution.py:121
  132.6 6.0 %gather_fusion.4 = bf16[28,128,768]{2,1,0:T(8,128)(2,1)} fusion(bf16[28,128,768]{2,1,0:T(8,128)(2,1)} %pad_maximum_fusion, s32[1024]{0:T(1024)S(1)} %pad_clamp_fusion), kind=kCustom, calls=%fused_computation.4 | custom fusion | bytes 11010160 | tf_op jit(solution)/shard_map/jit(_take)/gather | solution.py:134
  138.6 3.6 fusion.7
  143.9 32.1 %all_gather.15 = f32[256,768]{1,0:T(8,128)S(1)} all-gather(f32[32,768]{1,0:T(8,128)S(1)} %broadcast_divide_fusion.1), channel_id=1, replica_groups=mesh['grp'=4,'dev'=8] {'dev'}, dimensions={0}, use_global_device_ids=true | all-gather | bytes 884736 | tf_op jit(solution)/shard_map/all_gather | solution.py:144
  178.0 19.6 %psum.35 = f32[256]{0:T(256)S(1)} all-reduce(f32[256]{0:T(256)S(1)} %get-tuple-element.6), channel_id=1, replica_groups=mesh['grp'=4,'dev'=8] {'dev'}, use_global_device_ids=true, to_apply=%region_10.11 | all-reduce | flops 256 | bytes 2048 | tf_op jit(solution)/shard_map/psum | solution.py:152
  197.6 5.6 %psum.36 = f32[128]{0:T(128)S(1)} all-reduce(f32[128]{0:T(128)S(1)} %get-tuple-element.5), channel_id=1, replica_groups=mesh['grp'=4,'dev'=8] {'grp'}, use_global_device_ids=true, to_apply=%region_13.14 | all-reduce | flops 128 | bytes 1024 | tf_op jit(solution)/shard_map/psum | solution.py:153
  203.3 2.3 convolution_multiply_fusion.1
  205.7 2.8 convolution_multiply_fusion
  209.4 3.4 all-to-all-start.2
  216.5 40.7 %all-reduce.1 = (f32[]{:T(128)}, f32[]{:T(128)}) all-reduce(f32[]{:T(128)S(6)} %add.310, f32[]{:T(128)} %get-tuple-element.4), channel_id=1, replica_groups=mesh['grp'=4,'dev'=8] {'grp','dev'}, use_global_device_ids=true, to_apply=%region_15.16 | all-reduce | flops 2 | bytes 16 | tf_op jit(solution)/shard_map/psum | solution.py:171
  261.2 29.5 %reduce-scatter.3.cloned.1.call-done = f32[32,768]{1,0:T(8,128)} async-done(((f32[256,768]{1,0:T(8,128)}), f32[32,768]{1,0:T(8,128)}) %reduce-scatter.3.cloned.1.call-update) | async-done | bytes 98320 | tf_op jit(solution)/shard_map/reduce_scatter | solution.py:163
  291.9 4.4 fusion.57
  298.5 6.1 %fusion.12 = f32[28,128,768]{2,1,0:T(8,128)} fusion(bf16[28,32,128]{2,1,0:T(8,128)(2,1)S(1)} %bitcast_select_fusion.2, pred[28]{0:T(512)(128)(4,1)S(1)} %get-tuple-element.14, bf16[32,768]{1,0:T(8,128)(2,1)S(1)} %get-tuple-element.34), kind=kOutput, calls=%fused_computation.28 | convolution fusion | flops 176275456 | bytes 11288604 | tf_op jit(solution)/shard_map/tkc,kd->tcd/dot_general | solution.py:187
  305.9 25.6 %scatter_fusion = f32[4,128,768]{2,1,0:T(8,128)} fusion(f32[4,128,768]{2,1,0:T(8,128)} %broadcast_in_dim.214, s32[28]{0:T(128)S(1)} %get-tuple-element.15, f32[28,128,768]{2,1,0:T(8,128)} %fusion.12), kind=kCustom, calls=%fused_computation.5 | custom fusion | flops 2752512 | bytes 33030256 | tf_op jit(solution)/shard_map/scatter-add | solution.py:190
  331.5 31.1 %all_gather.18 = bf16[256,768]{1,0:T(8,128)(2,1)S(1)} all-gather(bf16[32,768]{1,0:T(8,128)(2,1)S(1)} %get-tuple-element.34), channel_id=1, replica_groups=mesh['grp'=4,'dev'=8] {'dev'}, dimensions={0}, use_global_device_ids=true | all-gather | bytes 442368 | tf_op jit(solution)/shard_map/all_gather | solution.py:198
  362.5 3.3 all-to-all-start.3
  366.9 3.4 bitcast_select_fusion
  370.2 14.6 %scatter_fusion.1 = f32[4,128,768]{2,1,0:T(8,128)} fusion(f32[4,128,768]{2,1,0:T(8,128)} %scatter_fusion, s32[16]{0:T(128)S(1)} %fusion.47, f32[16,128,768]{2,1,0:T(8,128)} %bitcast_select_fusion), kind=kCustom, calls=%fused_computation.6 | custom fusion | flops 1572864 | bytes 18874432 | tf_op jit(solution)/shard_map/scatter-add | solution.py:47
  384.9 6.0 %all_gather.19 = bf16[128,768]{1,0:T(8,128)(2,1)S(1)} all-gather(bf16[32,768]{1,0:T(8,128)(2,1)S(1)} %get-tuple-element.34), channel_id=1, replica_groups=mesh['grp'=4,'dev'=8] {'grp'}, dimensions={0}, use_global_device_ids=true | all-gather | bytes 245760 | tf_op jit(solution)/shard_map/all_gather | solution.py:214
  393.6 7.5 %scatter_fusion.2 = f32[4,128,768]{2,1,0:T(8,128)} fusion(f32[4,128,768]{2,1,0:T(8,128)} %scatter_fusion.1, s32[8]{0:T(128)S(1)} %fusion.48, f32[8,128,768]{2,1,0:T(8,128)} %bitcast_select_fusion.1), kind=kCustom, calls=%fused_computation.7 | custom fusion | flops 786432 | bytes 9437216 | tf_op jit(solution)/shard_map/scatter-add | solution.py:47
  401.1 3.4 scatter_fusion.3
  404.5 27.5 %all-reduce.4.cloned.1.call-done = f32[768,768]{1,0:T(8,128)} async-done(((f32[768,768]{1,0:T(8,128)}), f32[768,768]{1,0:T(8,128)}) %all-reduce.4.cloned.1.call-update) | async-done | bytes 2359312 | tf_op jit(solution)/shard_map/psum | solution.py:183
  432.0 3.2 copy.43
  (110 shorter events, 30.8 us)
Async XLA Ops:
  7.2 135.0 %copy-start = (f32[768,768]{1,0:T(8,128)S(1)}, f32[768,768]{1,0:T(8,128)}, u32[]{:S(2)}) copy-start(f32[768,768]{1,0:T(8,128)} %param.10) | copy-start | bytes 7077892
  15.3 25.1 %all-to-all-start.1 = ((bf16[4,2,128,768]{3,2,1,0:T(8,128)(2,1)}), bf16[4,2,128,768]{3,2,1,0:T(8,128)(2,1)}, u32[]{:S(2)}, u32[]{:S(2)}) async-start(bf16[4,2,128,768]{3,2,1,0:T(8,128)(2,1)} %select_select_fusion.1), calls=%async_computation.1 | async-start | bytes 3145728 | tf_op jit(solution)/shard_map/all_to_all | solution.py:114
  27.9 19.4 %copy-start.8 = (s32[32]{0:T(128)S(1)}, s32[32]{0:T(128)}, u32[]{:S(2)}) copy-start(s32[32]{0:T(128)} %param.12) | copy-start | bytes 388
  27.9 21.5 %copy-start.10 = (u32[32]{0:T(128)S(1)}, u32[32]{0:T(128)}, u32[]{:S(2)}) copy-start(u32[32]{0:T(128)} %constant.215) | copy-start | bytes 388
  27.9 25.5 %copy-start.9 = (s32[32]{0:T(128)S(1)}, s32[32]{0:T(128)}, u32[]{:S(2)}) copy-start(s32[32]{0:T(128)} %param.13) | copy-start | bytes 388
  27.9 90.8 %copy-start.3 = (f32[32,768]{1,0:T(8,128)S(1)}, f32[32,768]{1,0:T(8,128)}, u32[]{:S(2)}) copy-start(f32[32,768]{1,0:T(8,128)} %param.11) | copy-start | bytes 294916
  40.4 86.4 %all-to-all-start = ((bf16[8,2,128,768]{3,2,1,0:T(8,128)(2,1)}), bf16[8,2,128,768]{3,2,1,0:T(8,128)(2,1)}, u32[]{:S(2)}, u32[]{:S(2)}) async-start(bf16[8,2,128,768]{3,2,1,0:T(8,128)(2,1)} %select_select_fusion), calls=%async_computation | async-start | bytes 6291456 | tf_op jit(solution)/shard_map/all_to_all | solution.py:106
  47.1 211.4 %reduce-scatter.5.cloned.1.call-start = ((), (), s32[]{:S(2)}) async-start(), calls=%async_computation.8 | async-start | bytes 491520 | tf_op jit(solution)/shard_map/reduce_scatter | solution.py:167
  142.2 35.8 %copy-start.6 = (f32[32,768]{1,0:T(8,128)}, f32[32,768]{1,0:T(8,128)S(1)}, u32[]{:S(2)}) copy-start(f32[32,768]{1,0:T(8,128)S(1)} %fusion.7) | copy-start | bytes 294916
  142.2 33.8 %copy-start.2 = (f32[128,768]{1,0:T(8,128)S(1)}, f32[128,768]{1,0:T(8,128)}, u32[]{:S(2)}) copy-start(f32[128,768]{1,0:T(8,128)} %all_gather.16) | copy-start | bytes 1179652
  205.6 52.9 %copy-start.4 = (f32[32,768]{1,0:T(8,128)S(1)}, f32[32,768]{1,0:T(8,128)}, u32[]{:S(2)}) copy-start(f32[32,768]{1,0:T(8,128)} %param.11) | copy-start | bytes 294916
  205.6 86.2 %copy-start.7 = (f32[32,768]{1,0:T(8,128)S(1)}, f32[32,768]{1,0:T(8,128)}, u32[]{:S(2)}) copy-start(f32[32,768]{1,0:T(8,128)} %copy-done.6) | copy-start | bytes 294916
  205.6 85.1 %reduce-scatter.3.cloned.1.call-start = ((), (), s32[]{:S(2)}) async-start(), calls=%async_computation.6 | async-start | bytes 884736 | tf_op jit(solution)/shard_map/reduce_scatter | solution.py:163
  209.4 153.1 %all-to-all-start.2 = ((bf16[8,2,32,128]{3,2,1,0:T(8,128)(2,1)}), bf16[8,2,32,128]{3,2,1,0:T(8,128)(2,1)S(1)}, u32[]{:S(2)}, u32[]{:S(2)}) async-start(bf16[8,2,32,128]{3,2,1,0:T(8,128)(2,1)} %copy.27), calls=%async_computation.3 | async-start | bytes 262144 | tf_op jit(solution)/shard_map/all_to_all | solution.py:191
  212.8 219.2 %all-reduce.4.cloned.1.call-start = ((), (), s32[]{:S(2)}) async-start(), calls=%async_computation.7 | async-start | bytes 4718592 | tf_op jit(solution)/shard_map/psum | solution.py:183
  290.7 5.6 %copy-start.5 = (f32[32,768]{1,0:T(8,128)S(1)}, f32[32,768]{1,0:T(8,128)}, u32[]{:S(2)}) copy-start(f32[32,768]{1,0:T(8,128)} %reduce-scatter.3.cloned.1.call-done) | copy-start | bytes 294916
  362.5 28.4 %all-to-all-start.3 = ((bf16[4,2,32,128]{3,2,1,0:T(8,128)(2,1)}), bf16[4,2,32,128]{3,2,1,0:T(8,128)(2,1)S(1)}, u32[]{:S(2)}, u32[]{:S(2)}) async-start(bf16[4,2,32,128]{3,2,1,0:T(8,128)(2,1)} %copy.30), calls=%async_computation.4 | async-start | bytes 131072 | tf_op jit(solution)/shard_map/all_to_all | solution.py:207
  401.1 34.2 %copy-start.1 = (f32[768,768]{1,0:T(8,128)S(1)}, f32[768,768]{1,0:T(8,128)}, u32[]{:S(2)}) copy-start(f32[768,768]{1,0:T(8,128)} %param.10) | copy-start | bytes 7077892
Sparse Core Ops, SparseCore 0:
  205.7 17.4 reduce-scatter.4
  227.1 63.5 reduce-scatter.2
  296.8 135.1 all-reduce.3
where the time goes:
time: 445 us; the launch traced here: 443 us
  blocking collectives  206 us (46%)
  other arithmetic  78.9 us (18%)
  waiting for transfers between devices  69.5 us (16%)
  matrix products  27 us (6%)
  local copies, waits for them, and re-layouts  25.3 us (6%)
  between operations  18.5 us (4%)
  starting transfers between devices  17.8 us (4%)
    unnamed x1, blocking collectives  64.1 us
    psum x1, blocking collectives, shards(): lax.psum((jnp.sum(jnp.log(own_rows)) + jnp.sum(jnp.log(own_cols)), positi...  40.7 us
    all_gather x1, blocking collectives, shards(): lax.all_gather(unit_nodes, 'dev', axis=0, tiled=True)  32.1 us
    all_gather x1, blocking collectives, shards(): lax.all_gather(rounded_grads, 'dev', axis=0, tiled=True)  31.1 us
    reduce_scatter x1, waiting for transfers between devices, shards(): lax.psum_scatter(node_part, 'dev', scatter_dimension=0, tiled=True)  29.5 us
    psum x1, waiting for transfers between devices, shards(): grad_weight = lax.psum(weight_term, ('grp', 'dev'))  27.5 us
    scatter-add x1, other arithmetic, shards(): grad_blocks = empty_blocks.at[col_block].add(local_spread)  25.6 us
    scatter-add x2, other arithmetic, land_blocks(): total.at[block_index].add(jnp.where(valid[:, None, None], incoming, 0.0))  22.1 us
  transfers between devices with their start and end apart: 7, of which 3 were waited for; matrix products, arithmetic and copies ran while one was open for 22% of the time, Pallas kernels for 0%

commit v1 on v0

v1 whole, which is shorter than its diff:
```python
import functools

import jax
import jax.numpy as jnp
from jax import lax
from jax.experimental import pallas as pl
from jax.experimental.pallas import tpu as pltpu
from jax.sharding import PartitionSpec as P

CAP = 2


SCALE = 1.0 / 0.07
EPS = 1e-06
PRECISE = lax.Precision.HIGHEST
ROOT_HALF = 0.7071067811865476
INV_ROOT_TWO_PI = 0.3989422804014327
VMEM_SPEC = pl.BlockSpec(memory_space=pltpu.VMEM)
SMEM_SPEC = pl.BlockSpec(memory_space=pltpu.SMEM)


def gelu_value(value):
    return 0.5 * value * (1.0 + lax.erf(value * ROOT_HALF))


def gelu_slope(value):
    return (
        0.5 * (1.0 + lax.erf(value * ROOT_HALF))
        + value * jnp.exp(-0.5 * value * value) * INV_ROOT_TWO_PI
    )


def place():
    members = lax.axis_size("dev")
    return lax.axis_index("grp"), lax.axis_index("dev"), members


def pick_kernel(blocks_dev, flat, sel, pair, tiles, near, far, rows, selm, count, where_to):
    grp, dev, members = place()
    device = grp * members + dev
    tile_dev, block_rows, _ = tiles.shape
    sel_dev = selm.shape[0]
    base = device * blocks_dev * block_rows
    lane = lax.broadcasted_iota(jnp.int32, (1, block_rows), 1)
    coded = jnp.zeros((1, block_rows), jnp.int32)
    for k in range(sel_dev):
        selm[k : k + 1, :] = (sel[k] - base) - lane
        coded = jnp.where(lane == k, pair[k], coded)
    near[...] = jnp.zeros_like(near)
    far[...] = jnp.zeros_like(far)
    for i in range(count.shape[0]):
        count[i] = 0
    offsets = selm[...]
    for t in range(tile_dev):
        row_block = flat[2 * (device * tile_dev + t)] - device * blocks_dev
        hot = (offsets == row_block * block_rows).astype(jnp.bfloat16)
        rows[t] = jnp.dot(hot, tiles[t], preferred_element_type=jnp.float32).astype(jnp.bfloat16)
    high = coded // block_rows
    high_row = high.astype(jnp.float32).astype(jnp.bfloat16)
    low_row = (coded - high * block_rows).astype(jnp.float32).astype(jnp.bfloat16)
    for q in range(near.shape[0]):
        near[q, CAP, 0:1, :] = high_row
        near[q, CAP, 1:2, :] = low_row

    def step(t, carry):
        owner = flat[2 * (device * tile_dev + t) + 1] // blocks_dev
        rank = count[owner]
        count[owner] = rank + 1
        owner_grp = owner // members
        owner_dev = owner - owner_grp * members

        @pl.when((owner_grp == grp) & (owner_dev != dev))
        def _():
            near[owner_dev, rank] = rows[t]

        @pl.when(owner_grp != grp)
        def _():
            far[owner_grp, rank] = rows[t]

        return carry

    lax.fori_loop(0, tile_dev, step, 0)


def local_kernel(flat, sel, feats, rows, blocks, local, index):
    grp, dev, members = place()
    groups = lax.axis_size("grp")
    device = grp * members + dev
    blocks_dev, block_rows, _ = blocks.shape
    tile_dev, sel_dev, _ = rows.shape
    base = device * blocks_dev * block_rows
    for c in range(blocks_dev):
        blocks[c] = feats[c * block_rows : (c + 1) * block_rows, :].astype(jnp.bfloat16)
    for k in range(sel_dev):
        local[k : k + 1, :] = feats[pl.ds(sel[k] - base, 1), :]

    def add_tile(t, carry):
        column = flat[2 * (device * tile_dev + t) + 1]

        @pl.when(column // blocks_dev == device)
        def _():
            local[...] += jnp.dot(
                rows[t], blocks[column - device * blocks_dev], preferred_element_type=jnp.float32
            )

        return carry

    lax.fori_loop(0, tile_dev, add_tile, 0)
    for i in range(index.shape[0]):
        index[i] = 0
    for q in range(members + groups):
        peer = grp * members + q if q < members else (q - members) * members + dev

        def scan(t, hits, q=q, peer=peer):
            column = flat[2 * (peer * tile_dev + t) + 1]
            mine = column // blocks_dev == device
            index[q * (CAP + 1) + hits] = jnp.clip(column - device * blocks_dev, 0, blocks_dev - 1)
            return jnp.minimum(hits + mine.astype(jnp.int32), CAP)

        lax.fori_loop(0, tile_dev, scan, 0)


def partial_kernel(index, near_in, far_in, blocks, local, near_part, far_part):
    _, dev, members = place()
    groups = far_in.shape[0]
    for q in range(members + groups):
        source = near_in if q < members else far_in
        target = near_part if q < members else far_part
        p = q if q < members else q - members
        total = jnp.dot(
            source[p, 0], blocks[index[q * (CAP + 1)]], preferred_element_type=jnp.float32
        )
        for s in range(1, CAP):
            total += jnp.dot(
                source[p, s], blocks[index[q * (CAP + 1) + s]], preferred_element_type=jnp.float32
            )
        target[p] = total
    near_part[dev] = local[...]


def spread_kernel(
    blocks_dev, flat, sel, index, near_in, far_in, rows, near_grads, far_grads, row_grads, out
):
    grp, dev, members = place()
    device = grp * members + dev
    groups = far_in.shape[0]
    tile_dev, sel_dev, block_rows = rows.shape
    base = device * blocks_dev * block_rows
    across = (((0,), (0,)), ((), ()))
    out[...] = jnp.zeros_like(out)
    for q in range(members + groups):
        source = near_in if q < members else far_in
        grads = near_grads if q < members else far_grads
        p = q if q < members else q - members
        for s in range(CAP):
            c = index[q * (CAP + 1) + s]
            span = pl.ds(pl.multiple_of(c * block_rows, block_rows), block_rows)
            out[span, :] += lax.dot_general(
                source[p, s], grads[p], across, preferred_element_type=jnp.float32
            )
    own = near_grads[dev]

    def add_tile(t, carry):
        column = flat[2 * (device * tile_dev + t) + 1]

        @pl.when(column // blocks_dev == device)
        def _():
            c = column - device * blocks_dev
            span = pl.ds(pl.multiple_of(c * block_rows, block_rows), block_rows)
            out[span, :] += lax.dot_general(
                rows[t], own, across, preferred_element_type=jnp.float32
            )

        return carry

    lax.fori_loop(0, tile_dev, add_tile, 0)
    for k in range(sel_dev):
        out[pl.ds(sel[k] - base, 1), :] += row_grads[k : k + 1, :]


def split_size(count):
    return next(n for n in (4, 2, 1) if count % n == 0)


def gather_axis(part, axis, outer, inner, outer_first=True):
    def shift(value, do, di):
        pairs = [
            (((o + do) % outer) * inner + (i + di) % inner, o * inner + i)
            for o in range(outer)
            for i in range(inner)
        ]
        return lax.ppermute(value, axis, pairs)

    stage = jnp.stack([part] + [shift(part, j, 0) for j in range(1, outer)])
    return jnp.stack([stage] + [shift(stage, 0, j) for j in range(1, inner)])


def offsets(index, outer, inner):
    o = (index // inner + jnp.arange(outer, dtype=jnp.int32)) % outer
    i = (index % inner + jnp.arange(inner, dtype=jnp.int32)) % inner
    return o[None, :] * inner + i[:, None]


def shards(node_features, tiles, tile_list, weight, texts, selected, pairing):
    groups = lax.axis_size("grp")
    members = lax.axis_size("dev")
    grp_index = lax.axis_index("grp")
    dev_index = lax.axis_index("dev")
    block_rows = tiles.shape[1]
    feat_width = node_features.shape[1]
    blocks_dev = node_features.shape[0] // block_rows
    tile_dev = tiles.shape[0]
    sel_dev = selected.shape[0]
    total_sel = sel_dev * groups * members
    group_sel = sel_dev * members
    f32 = jnp.float32
    grp_inner = 2 if groups % 2 == 0 else 1
    grp_outer = groups // grp_inner
    dev_outer = split_size(members)
    dev_inner = members // dev_outer
    flat = tile_list.reshape(-1)

    near_rows, far_rows, tile_rows = pl.pallas_call(
        functools.partial(pick_kernel, blocks_dev),
        out_shape=(
            jax.ShapeDtypeStruct((members, CAP + 1, sel_dev, block_rows), jnp.bfloat16),
            jax.ShapeDtypeStruct((groups, CAP, sel_dev, block_rows), jnp.bfloat16),
            jax.ShapeDtypeStruct((tile_dev, sel_dev, block_rows), jnp.bfloat16),
        ),
        in_specs=[SMEM_SPEC, SMEM_SPEC, SMEM_SPEC, VMEM_SPEC],
        out_specs=(VMEM_SPEC, VMEM_SPEC, VMEM_SPEC),
        scratch_shapes=[
            pltpu.VMEM((sel_dev, block_rows), jnp.int32),
            pltpu.SMEM((groups * members,), jnp.int32),
            pltpu.SMEM((8,), jnp.int32),
        ],
        cost_estimate=pl.CostEstimate(flops=2 * 10**6, bytes_accessed=10**6, transcendentals=0),
        name="pick",
    )(flat, selected, pairing, tiles)
    near_in = lax.all_to_all(near_rows, "dev", 0, 0, tiled=True)
    far_in = lax.all_to_all(far_rows, "grp", 0, 0, tiled=True)

    text_norm = jnp.sqrt(jnp.sum(texts * texts, axis=1, keepdims=True) + EPS)
    unit_texts = texts / text_norm
    text_near = gather_axis(unit_texts, "dev", dev_outer, dev_inner).reshape(group_sel, feat_width)
    text_all = gather_axis(text_near, "grp", grp_outer, grp_inner).reshape(total_sel, feat_width)
    grp_of = offsets(grp_index, grp_outer, grp_inner).reshape(-1)
    dev_of = offsets(dev_index, dev_outer, dev_inner).reshape(-1)
    text_id = (
        (grp_of[:, None, None] * members + dev_of[None, :, None]) * sel_dev
        + jnp.arange(sel_dev, dtype=jnp.int32)[None, None, :]
    ).reshape(-1)

    blocks, local, index = pl.pallas_call(
        local_kernel,
        out_shape=(
            jax.ShapeDtypeStruct((blocks_dev, block_rows, feat_width), jnp.bfloat16),
            jax.ShapeDtypeStruct((sel_dev, feat_width), f32),
            jax.ShapeDtypeStruct(((members + groups) * (CAP + 1),), jnp.int32),
        ),
        in_specs=[SMEM_SPEC, SMEM_SPEC, VMEM_SPEC, VMEM_SPEC],
        out_specs=(VMEM_SPEC, VMEM_SPEC, SMEM_SPEC),
        cost_estimate=pl.CostEstimate(flops=2 * 10**6, bytes_accessed=10**6, transcendentals=0),
        name="local",
    )(flat, selected, node_features, tile_rows)
    near_part, far_part = pl.pallas_call(
        partial_kernel,
        out_shape=(
            jax.ShapeDtypeStruct((members, sel_dev, feat_width), f32),
            jax.ShapeDtypeStruct((groups, sel_dev, feat_width), f32),
        ),
        in_specs=[SMEM_SPEC, VMEM_SPEC, VMEM_SPEC, VMEM_SPEC, VMEM_SPEC],
        out_specs=(VMEM_SPEC, VMEM_SPEC),
        cost_estimate=pl.CostEstimate(flops=2 * 10**6, bytes_accessed=10**6, transcendentals=0),
        name="partial",
    )(index, near_in, far_in, blocks, local)
    near_back = lax.all_to_all(near_part, "dev", 0, 0, tiled=True)
    far_back = lax.all_to_all(far_part, "grp", 0, 0, tiled=True)
    own_chosen = jnp.sum(near_back, axis=0) + jnp.sum(far_back, axis=0)

    chosen = lax.all_to_all(
        jnp.broadcast_to(own_chosen[None], (members, sel_dev, feat_width)), "dev", 0, 0, tiled=True
    ).reshape(group_sel, feat_width)
    chosen_all = gather_axis(chosen, "grp", grp_outer, grp_inner).reshape(total_sel, feat_width)
    coded = near_in[:, CAP, :2, :sel_dev].astype(jnp.int32)
    pair_rows = (coded[:, 0, :] * block_rows + coded[:, 1, :]).reshape(-1)

    before = jnp.dot(chosen, weight, precision=PRECISE)
    hidden = gelu_value(before)
    node_norm = jnp.sqrt(jnp.sum(hidden * hidden, axis=1, keepdims=True) + EPS)
    unit_nodes = hidden / node_norm
    scores = SCALE * lax.dot_general(
        unit_nodes, text_all, (((1,), (1,)), ((), ())), precision=PRECISE
    )
    target = pair_rows[:, None] == text_id[None, :]
    exp_scores = jnp.exp(scores)
    row_total = jnp.sum(exp_scores, axis=1)
    positive = jnp.sum(jnp.where(target, scores, 0.0))
    col_part = jnp.sum(exp_scores, axis=0).reshape(groups, group_sel)
    is_grp = grp_of[:, None] == jnp.arange(groups, dtype=jnp.int32)[None, :]
    col_ordered = jnp.sum(jnp.where(is_grp[:, :, None], col_part[:, None, :], 0.0), axis=0)
    lane = jnp.arange(group_sel, dtype=jnp.int32)
    sums = jnp.where(
        lane == 0, jnp.sum(jnp.log(row_total)), jnp.where(lane == 1, positive, 0.0)
    )
    totals = lax.psum(jnp.concatenate([col_ordered, sums[None, :]], axis=0), "grp")
    col_total = jnp.sum(
        jnp.where(is_grp[:, :, None], totals[None, :groups, :], 0.0), axis=1
    ).reshape(-1)
    contrast_loss = (totals[groups, 0] + jnp.sum(jnp.log(col_total))) / (
        2.0 * total_sel
    ) - totals[groups, 1] / total_sel

    score_grads = 0.5 * (
        exp_scores / row_total[:, None] + exp_scores / col_total[None, :]
    ) - target.astype(f32)
    node_dir = SCALE * jnp.dot(score_grads, text_all, precision=PRECISE)
    node_back = (
        node_dir - unit_nodes * jnp.sum(unit_nodes * node_dir, axis=1, keepdims=True)
    ) / node_norm
    pre_grad = node_back * gelu_slope(before)
    pre_all = gather_axis(pre_grad, "grp", grp_outer, grp_inner).reshape(total_sel, feat_width)
    row_grads = lax.dot_general(pre_grad, weight, (((1,), (1,)), ((), ())), precision=PRECISE)
    near_grads = row_grads.astype(jnp.bfloat16).reshape(members, sel_dev, feat_width)
    own_grads = lax.dynamic_index_in_dim(
        row_grads.reshape(members, sel_dev, feat_width), dev_index, 0, False
    )
    far_grads = lax.all_gather(own_grads.astype(jnp.bfloat16), "grp", axis=0)
    grad_nodes = pl.pallas_call(
        functools.partial(spread_kernel, blocks_dev),
        out_shape=jax.ShapeDtypeStruct(node_features.shape, f32),
        in_specs=[SMEM_SPEC] * 3 + [VMEM_SPEC] * 6,
        out_specs=VMEM_SPEC,
        cost_estimate=pl.CostEstimate(flops=2 * 10**6, bytes_accessed=10**6, transcendentals=0),
        name="spread",
    )(flat, selected, index, near_in, far_in, tile_rows, near_grads, far_grads, own_grads)

    own_cols = score_grads.reshape(group_sel, groups, members, sel_dev)[:, :, 0, :]
    text_part = SCALE * lax.dot_general(
        own_cols.reshape(group_sel, groups * sel_dev),
        unit_nodes,
        (((0,), (0,)), ((), ())),
        precision=PRECISE,
    ).reshape(groups, sel_dev, feat_width)
    text_dir = text_part[0]
    for r in range(1, groups):
        di, do = r // grp_outer, r % grp_outer
        pairs = [
            (o * grp_inner + i, ((o + do) % grp_outer) * grp_inner + (i + di) % grp_inner)
            for o in range(grp_outer)
            for i in range(grp_inner)
        ]
        text_dir = text_dir + lax.ppermute(text_part[r], "grp", pairs)
    grad_texts = (
        text_dir - unit_texts * jnp.sum(unit_texts * text_dir, axis=1, keepdims=True)
    ) / text_norm

    grad_weight = lax.dot_general(
        chosen_all, pre_all, (((0,), (0,)), ((), ())), precision=PRECISE
    )
    return (contrast_loss, grad_nodes, grad_weight, grad_texts)


def solution(mesh):
    return jax.shard_map(
        shards,
        mesh=mesh,
        in_specs=(
            P(("grp", "dev"), None),
            P(("grp", "dev"), None, None),
            P(),
            P(),
            P(("grp", "dev"), None),
            P(("grp", "dev")),
            P(("grp", "dev")),
        ),
        out_specs=(P(), P(("grp", "dev"), None), P(), P(("grp", "dev"), None)),
        check_vma=False,
    )
```

time: 445 us -> 213 us (0.48)
  blocking collectives: 206 us -> 12.2 us
  other arithmetic: 78.9 us -> 28.3 us
  Pallas kernels: 0 us -> 25 us
  starting transfers between devices: 17.8 us -> 35.3 us
  local copies, waits for them, and re-layouts: 25.3 us -> 9.93 us
  between operations: 18.5 us -> 4.02 us
    all_gather x4 -> x1, blocking collectives: 75.8 us -> 6.26 us  [shards(): far_grads = lax.all_gather(own_grads.astype(jnp.bfloat16), 'grp', axis=0)]
    unnamed x1 -> x0, blocking collectives: 64.1 us -> none
    psum x3 -> x1, blocking collectives: 66 us -> 5.95 us  [shards(): lax.psum(jnp.concatenate([col_ordered, sums[None, :]], axis=0), 'grp')]
    scatter-add x4 -> x0, other arithmetic: 51.1 us -> none  [the longest x1 25.6 us: shards(): grad_blocks = empty_blocks.at[col_block].add(local_spread)]
    ppermute x0 -> x13, waiting for transfers between devices: none -> 37.4 us  [the longest x10 37.4 us: shift(): return lax.ppermute(value, axis, pairs)]
    reduce_scatter x2 -> x0, waiting for transfers between devices: 29.5 us -> none  [the longest x1 29.5 us: shards(): lax.psum_scatter(node_part, 'dev', scatter_dimension=0, tiled=True)]
    psum x1 -> x0, waiting for transfers between devices: 27.5 us -> none  [shards(): grad_weight = lax.psum(weight_term, ('grp', 'dev'))]
    pallas_call x0 -> x4, Pallas kernels: none -> 25 us  [the longest x1 11.2 us: shards(): pl.pallas_call(local_kernel, out_shape=(jax.ShapeDtypeStruct((blocks_dev,...]
  transfers between devices with their start and end apart: 7 -> 18, of which waited for: 3 -> 7; matrix products, arithmetic and copies ran while one was open for 22% -> 17% of each run, Pallas kernels for 0% -> 12%
where the time goes in v1:
time: 213 us; the launch traced here: 212 us
  waiting for transfers between devices  65.3 us (31%)
  starting transfers between devices  35.3 us (17%)
  matrix products  31.4 us (15%)
  other arithmetic  28.3 us (13%)
  Pallas kernels  25 us (12%)
  blocking collectives  12.2 us (6%)
  local copies, waits for them, and re-layouts  9.93 us (5%)
  between operations  4.02 us (2%)
    ppermute x10, waiting for transfers between devices, shift(): return lax.ppermute(value, axis, pairs)  37.4 us
    all_to_all x1, waiting for transfers between devices, shards(): lax.all_to_all(jnp.broadcast_to(own_chosen[None], (members, sel_dev, feat...  15.3 us
    another operation x6, other arithmetic, gather_axis(): return jnp.stack([stage] + [shift(stage, 0, j) for j in range(1, inner)])  15.3 us
    dot_general x1, matrix products, shards(): lax.dot_general(chosen_all, pre_all, (((0,), (0,)), ((), ())), precision=...  13.5 us
    ppermute x10, starting transfers between devices, shift(): return lax.ppermute(value, axis, pairs)  12.2 us
    pallas_call x1, Pallas kernels, shards(): pl.pallas_call(local_kernel, out_shape=(jax.ShapeDtypeStruct((blocks_dev,...  11.2 us
    pallas_call x1, Pallas kernels, shards(): pl.pallas_call(functools.partial(spread_kernel, blocks_dev), out_shape=ja...  7.67 us
    all_gather x1, blocking collectives, shards(): far_grads = lax.all_gather(own_grads.astype(jnp.bfloat16), 'grp', axis=0)  6.26 us
  transfers between devices with their start and end apart: 18, of which 7 were waited for; matrix products, arithmetic and copies ran while one was open for 17% of the time, Pallas kernels for 12%

profile of v1, /device:TPU:0, one launch (start us, length us, event | category | flops | bytes accessed | tf_op | source)
XLA Modules:
  0.0 211.5 jit_solution(12748794087584324420)
XLA Ops:
  3.5 5.1 %collective-permute-start = (f32[32,768]{1,0:T(8,128)}, f32[32,768]{1,0:T(8,128)S(1)}, u32[]{:S(2)}, u32[]{:S(2)}) collective-permute-start(f32[32,768]{1,0:T(8,128)} %broadcast_divide_fusion.1), channel_id=1, source_target_pairs={{2,0},{3,1},{4,2},{5,3},{6,4},{7,5},{0,6},{1,7},{10,8},{11,9},{12,... | collective-permute-start | bytes 294920 | tf_op jit(solution)/shard_map/ppermute | solution.py:192
  11.3 3.3 %pick.1 = (bf16[8,3,32,128]{3,2,1,0:T(8,128)(2,1)}, bf16[4,2,32,128]{3,2,1,0:T(8,128)(2,1)}, bf16[28,32,128]{2,1,0:T(8,128)(2,1)}) custom-call(s32[1792]{0:T(1024)} %reshape.267.flat, s32[32]{0:T(128)} %sel.5, s32[32]{0:T(128)} %pair.1, bf16[28,128,128]{2,1,0:T(8,128)(2,1)} %tiles.1), custom_call_target="tpu_custom_call" | custom-call | flops 2000000 | bytes 1000000 | tf_op jit(solution)/shard_map/pick/pallas_call | solution.py:223
  14.6 3.3 %all-to-all-start.1 = ((bf16[4,2,32,128]{3,2,1,0:T(8,128)(2,1)}), bf16[4,2,32,128]{3,2,1,0:T(8,128)(2,1)S(1)}, u32[]{:S(2)}, u32[]{:S(2)}) async-start(bf16[4,2,32,128]{3,2,1,0:T(8,128)(2,1)} %get-tuple-element.15), calls=%async_computation.1 | async-start | bytes 131072 | tf_op jit(solution)/shard_map/all_to_all | solution.py:241
  18.0 4.0 %all-to-all-done.1.far_in = bf16[4,2,32,128]{3,2,1,0:T(8,128)(2,1)S(1)} async-done(((bf16[4,2,32,128]{3,2,1,0:T(8,128)(2,1)}), bf16[4,2,32,128]{3,2,1,0:T(8,128)(2,1)S(1)}, u32[]{:S(2)}, u32[]{:S(2)}) %all-to-all-start.1) | async-done | bytes 65568 | tf_op jit(solution)/shard_map/all_to_all | solution.py:241
  22.0 5.0 %all-to-all-start = ((bf16[8,3,32,128]{3,2,1,0:T(8,128)(2,1)}), bf16[8,3,32,128]{3,2,1,0:T(8,128)(2,1)S(1)}, u32[]{:S(2)}, u32[]{:S(2)}) async-start(bf16[8,3,32,128]{3,2,1,0:T(8,128)(2,1)} %get-tuple-element.14), calls=%async_computation | async-start | bytes 393216 | tf_op jit(solution)/shard_map/all_to_all | solution.py:240
  27.8 2.0 collective-permute-start.3
  29.9 11.2 %local.1 = (bf16[4,128,768]{2,1,0:T(8,128)(2,1)}, f32[32,768]{1,0:T(8,128)}, s32[36]{0:T(128)}) custom-call(s32[1792]{0:T(1024)} %reshape.267.flat, s32[32]{0:T(128)} %sel.5, f32[512,768]{1,0:T(8,128)} %feats.1, bf16[28,32,128]{2,1,0:T(8,128)(2,1)} %get-tuple-element.12.rows), custom_call_target="tpu_custom_call" | custom-call | flops 2000000 | bytes 1000000 | tf_op jit(solution)/shard_map/local/pallas_call | solution.py:254
  41.8 2.9 %partial.1 = (f32[8,32,768]{2,1,0:T(8,128)}, f32[4,32,768]{2,1,0:T(8,128)}) custom-call(s32[36]{0:T(128)} %get-tuple-element.13.index, bf16[8,3,32,128]{3,2,1,0:T(8,128)(2,1)} %copy-done.8, bf16[4,2,32,128]{3,2,1,0:T(8,128)(2,1)} %copy-done.9, bf16[4,128,768]{2,1,0:T(8,128)(2,1)} %get-tuple-element.16.blocks, f32[32,768]{1,0:T(8,128)} %get-tuple-element.17.local), custom_call_target="tpu_custom_call" | custom-call | flops 2000000 | bytes 1000000 | tf_op jit(solution)/shard_map/partial/pallas_call | solution.py:266
  44.6 4.1 %all-to-all-start.3 = ((f32[4,32,768]{2,1,0:T(8,128)}), f32[4,32,768]{2,1,0:T(8,128)}, u32[]{:S(2)}, u32[]{:S(2)}) async-start(f32[4,32,768]{2,1,0:T(8,128)} %get-tuple-element.19), calls=%async_computation.3 | async-start | bytes 786432 | tf_op jit(solution)/shard_map/all_to_all | solution.py:278
  49.9 2.0 collective-permute-start.4
  52.0 4.8 %all-to-all-done.3 = f32[4,32,768]{2,1,0:T(8,128)} async-done(((f32[4,32,768]{2,1,0:T(8,128)}), f32[4,32,768]{2,1,0:T(8,128)}, u32[]{:S(2)}, u32[]{:S(2)}) %all-to-all-start.3) | async-done | bytes 393248 | tf_op jit(solution)/shard_map/all_to_all | solution.py:278
  56.8 5.0 %all-to-all-start.2 = ((f32[8,32,768]{2,1,0:T(8,128)}), f32[8,32,768]{2,1,0:T(8,128)}, u32[]{:S(2)}, u32[]{:S(2)}) async-start(f32[8,32,768]{2,1,0:T(8,128)} %get-tuple-element.18), calls=%async_computation.2 | async-start | bytes 1572864 | tf_op jit(solution)/shard_map/all_to_all | solution.py:277
  61.8 11.2 %collective-permute-done.4 = f32[256,768]{1,0:T(8,128)} collective-permute-done((f32[256,768]{1,0:T(8,128)S(1)}, f32[256,768]{1,0:T(8,128)}, u32[]{:S(2)}, u32[]{:S(2)}) %collective-permute-start.4) | collective-permute-done | bytes 786464 | tf_op jit(solution)/shard_map/ppermute | solution.py:192
  73.1 3.0 %fusion.35 = (f32[1,2,256,768]{3,2,1,0:T(8,128)}, f32[2,256,768]{2,1,0:T(8,128)}) fusion(f32[1,256,768]{2,1,0:T(8,128)} %bitcast.9, f32[1,256,768]{2,1,0:T(8,128)S(1)} %bitcast.82), kind=kLoop, calls=%fused_computation.91 | loop fusion | flops 393216 | bytes 4718592 | tf_op jit(solution)/shard_map/stack | solution.py:195
  77.4 3.8 %all-to-all-done.2 = f32[8,32,768]{2,1,0:T(8,128)} async-done(((f32[8,32,768]{2,1,0:T(8,128)}), f32[8,32,768]{2,1,0:T(8,128)}, u32[]{:S(2)}, u32[]{:S(2)}) %all-to-all-start.2) | async-done | bytes 786464 | tf_op jit(solution)/shard_map/all_to_all | solution.py:277
  83.4 3.5 %all-to-all-start.4 = ((f32[8,32,768]{2,1,0:T(8,128)}), f32[8,32,768]{2,1,0:T(8,128)S(1)}, u32[]{:S(2)}, u32[]{:S(2)}) async-start(f32[8,32,768]{2,1,0:T(8,128)} %broadcast_in_dim.76), calls=%async_computation.4 | async-start | bytes 1572864 | tf_op jit(solution)/shard_map/all_to_all | solution.py:281
  88.1 3.8 %pad_maximum_fusion = f32[2,2,256,768]{3,2,1,0:T(8,128)} fusion(f32[1,2,256,768]{3,2,1,0:T(8,128)} %bitcast.11, f32[1,2,256,768]{3,2,1,0:T(8,128)} %get-tuple-element.29), kind=kLoop, calls=%fused_computation | loop fusion | flops 786432 | bytes 6291456 | tf_op jit(solution)/shard_map/stack | solution.py:195
  91.9 15.3 %all-to-all-done.4 = f32[8,32,768]{2,1,0:T(8,128)S(1)} async-done(((f32[8,32,768]{2,1,0:T(8,128)}), f32[8,32,768]{2,1,0:T(8,128)S(1)}, u32[]{:S(2)}, u32[]{:S(2)}) %all-to-all-start.4) | async-done | bytes 786464 | tf_op jit(solution)/shard_map/all_to_all | solution.py:281
  107.3 2.3 %multiply_reduce_fusion.1 = (f32[256]{0:T(256)S(1)}, f32[256,768]{1,0:T(8,128)S(1)}) fusion(f32[256,768]{1,0:T(8,128)S(1)} %bitcast.76, f32[768,768]{1,0:T(8,128)S(1)} %copy-done), kind=kOutput, calls=%fused_computation.30 | convolution fusion | flops 1813118720 | bytes 3933184 | tf_op jit(solution)/shard_map/dot_general | solution.py:288
  109.6 4.6 %exponential_reduce_fusion.1 = (f32[1024]{0:T(1024)S(1)}, f32[256]{0:T(256)S(1)}, f32[]{:T(128)}, f32[256,1024]{1,0:T(8,128)}) fusion(s32[1024]{0:T(1024)S(1)} %add.271, s32[256]{0:T(256)S(1)} %add.253, f32[1024,768]{1,0:T(8,128)S(1)} %bitcast.80, f32[256]{0:T(256)S(1)} %add_sqrt_fusion, f32[256,768]{1,0:T(8,128)S(1)} %get-tuple-element.39), kind=kOutput, calls=%fused_computation.21 | convolution fusion | flops 2418473728 | bytes 4992004 | tf_op jit(solution)/shard_map/dot_general | solution.py:292
  116.2 5.9 %psum.7 = f32[5,256]{1,0:T(8,128)S(1)} all-reduce(f32[5,256]{1,0:T(8,128)S(1)} %pad_maximum_fusion.6), channel_id=1, replica_groups=mesh['grp'=4,'dev'=8] {'grp'}, use_global_device_ids=true, to_apply=%region_9.10 | all-reduce | flops 1280 | bytes 10240 | tf_op jit(solution)/shard_map/psum | solution.py:306
  124.0 5.3 %multiply_reduce_fusion = (f32[256]{0:T(256)S(1)}, f32[256,768]{1,0:T(8,128)S(1)}) fusion(f32[256]{0:T(256)S(1)} %add_sqrt_fusion, f32[256,768]{1,0:T(8,128)S(1)} %copy-done.4, f32[256,1024]{1,0:T(8,128)S(1)} %fusion.13, f32[1024,768]{1,0:T(8,128)} %bitcast.79), kind=kOutput, calls=%fused_computation.29 | convolution fusion | flops 2417491712 | bytes 5769216 | tf_op jit(solution)/shard_map/dot_general | solution.py:317
  133.9 2.6 %copy.23 = f32[256,1024]{0,1:T(8,128)} copy(f32[256,1024]{1,0:T(8,128)} %copy-done.2) | data formatting | bytes 2097152 | tf_op jit(solution)/shard_map/sub | solution.py:314
  137.7 13.8 %collective-permute-done.8 = f32[256,768]{1,0:T(8,128)} collective-permute-done((f32[256,768]{1,0:T(8,128)}, f32[256,768]{1,0:T(8,128)}, u32[]{:S(2)}, u32[]{:S(2)}) %collective-permute-start.8) | collective-permute-done | bytes 786464 | tf_op jit(solution)/shard_map/ppermute | solution.py:192
  151.4 3.4 %fusion.33 = (f32[1,2,256,768]{3,2,1,0:T(8,128)}, f32[2,256,768]{2,1,0:T(8,128)}) fusion(f32[1,256,768]{2,1,0:T(8,128)} %bitcast.25, f32[1,256,768]{2,1,0:T(8,128)} %bitcast.24), kind=kLoop, calls=%fused_computation.89 | loop fusion | flops 393216 | bytes 4718592 | tf_op jit(solution)/shard_map/stack | solution.py:195
  154.8 12.3 %collective-permute-done.6 = f32[256,768]{0,1:T(8,128)} collective-permute-done((f32[256,768]{0,1:T(8,128)}, f32[256,768]{0,1:T(8,128)}, u32[]{:S(2)}, u32[]{:S(2)}) %collective-permute-start.6) | collective-permute-done | bytes 786464 | tf_op jit(solution)/shard_map/ppermute | solution.py:192
  167.2 3.1 %fusion.34 = (f32[1,2,256,768]{2,3,1,0:T(8,128)}, f32[2,256,768]{1,2,0:T(8,128)}) fusion(f32[1,256,768]{1,2,0:T(8,128)} %bitcast.21, f32[1,256,768]{1,2,0:T(8,128)S(1)} %copy-done.6), kind=kLoop, calls=%fused_computation.90 | loop fusion | flops 393216 | bytes 4718592 | tf_op jit(solution)/shard_map/stack | solution.py:195
  170.2 1.6 convolution_multiply_fusion.2
  177.3 4.1 %fusion.38 = (bf16[256,768]{1,0:T(8,128)(2,1)}, f32[256,768]{1,0:T(8,128)S(1)}) fusion(f32[256,768]{1,0:T(8,128)} %fusion.18, f32[768,768]{1,0:T(8,128)S(1)} %copy-done), kind=kOutput, calls=%fused_computation.93 | convolution fusion | flops 1812135936 | bytes 4325376 | tf_op jit(solution)/shard_map/dot_general | solution.py:323
  181.3 6.3 %all_gather.4.far_grads = bf16[4,32,768]{2,1,0:T(8,128)(2,1)} all-gather(bf16[1,32,768]{2,1,0:T(8,128)(2,1)S(1)} %dynamic-slice_convert_fusion), channel_id=1, replica_groups=mesh['grp'=4,'dev'=8] {'grp'}, dimensions={0}, use_global_device_ids=true | all-gather | bytes 245760 | tf_op jit(solution)/shard_map/all_gather | solution.py:328
  188.2 7.7 %spread.1 = f32[512,768]{1,0:T(8,128)} custom-call(s32[1792]{0:T(1024)} %reshape.267.flat, s32[32]{0:T(128)} %sel.5, s32[36]{0:T(128)} %get-tuple-element.13.index, bf16[8,3,32,128]{3,2,1,0:T(8,128)(2,1)} %copy-done.8, bf16[4,2,32,128]{3,2,1,0:T(8,128)(2,1)} %copy-done.9, bf16[28,32,128]{2,1,0:T(8,128)(2,1)} %get-tuple-element.12.rows, ...), custom_call_target="tpu_custom_call" | custom-call | flops 2000000 | bytes 1000000 | tf_op jit(solution)/shard_map/spread/pallas_call | solution.py:329
  196.9 13.5 %fusion.7 = f32[768,768]{1,0:T(8,128)} fusion(f32[1,2,256,768]{3,2,1,0:T(8,128)} %bitcast.27, f32[1,2,256,768]{3,2,1,0:T(8,128)} %get-tuple-element.27, f32[1,2,256,768]{2,3,1,0:T(8,128)} %bitcast.23, f32[1,2,256,768]{2,3,1,0:T(8,128)} %get-tuple-element.25), kind=kOutput, calls=%fused_computation.8 | convolution fusion | flops 7249330176 | bytes 8650752 | tf_op jit(solution)/shard_map/dot_general | solution.py:358
  (88 shorter events, 27.5 us)
Async XLA Ops:
  0.6 106.7 %copy-start = (f32[768,768]{1,0:T(8,128)S(1)}, f32[768,768]{1,0:T(8,128)}, u32[]{:S(2)}) copy-start(f32[768,768]{1,0:T(8,128)} %param.10) | copy-start | bytes 7077892
  0.6 17.2 %copy-start.7 = (f32[32,768]{1,0:T(8,128)S(1)}, f32[32,768]{1,0:T(8,128)}, u32[]{:S(2)}) copy-start(f32[32,768]{1,0:T(8,128)} %param.11) | copy-start | bytes 294916
  3.5 23.5 %collective-permute-start = (f32[32,768]{1,0:T(8,128)}, f32[32,768]{1,0:T(8,128)S(1)}, u32[]{:S(2)}, u32[]{:S(2)}) collective-permute-start(f32[32,768]{1,0:T(8,128)} %broadcast_divide_fusion.1), channel_id=1, source_target_pairs={{2,0},{3,1},{4,2},{5,3},{6,4},{7,5},{0,6},{1,7},{10,8},{11,9},{12,... | collective-permute-start | bytes 294920 | tf_op jit(solution)/shard_map/ppermute | solution.py:192
  8.5 18.5 %collective-permute-start.1 = (f32[32,768]{1,0:T(8,128)}, f32[32,768]{1,0:T(8,128)S(1)}, u32[]{:S(2)}, u32[]{:S(2)}) collective-permute-start(f32[32,768]{1,0:T(8,128)} %broadcast_divide_fusion.1), channel_id=1, source_target_pairs={{4,0},{5,1},{6,2},{7,3},{0,4},{1,5},{2,6},{3,7},{12,8},{13,9},{14,... | collective-permute-start | bytes 294920 | tf_op jit(solution)/shard_map/ppermute | solution.py:192
  8.5 18.5 %collective-permute-start.2 = (f32[32,768]{1,0:T(8,128)}, f32[32,768]{1,0:T(8,128)S(1)}, u32[]{:S(2)}, u32[]{:S(2)}) collective-permute-start(f32[32,768]{1,0:T(8,128)} %broadcast_divide_fusion.1), channel_id=1, source_target_pairs={{6,0},{7,1},{0,2},{1,3},{2,4},{3,5},{4,6},{5,7},{14,8},{15,9},{8,1... | collective-permute-start | bytes 294920 | tf_op jit(solution)/shard_map/ppermute | solution.py:192
  14.6 7.4 %all-to-all-start.1 = ((bf16[4,2,32,128]{3,2,1,0:T(8,128)(2,1)}), bf16[4,2,32,128]{3,2,1,0:T(8,128)(2,1)S(1)}, u32[]{:S(2)}, u32[]{:S(2)}) async-start(bf16[4,2,32,128]{3,2,1,0:T(8,128)(2,1)} %get-tuple-element.15), calls=%async_computation.1 | async-start | bytes 131072 | tf_op jit(solution)/shard_map/all_to_all | solution.py:241
  22.0 19.1 %copy-start.9 = (bf16[4,2,32,128]{3,2,1,0:T(8,128)(2,1)}, bf16[4,2,32,128]{3,2,1,0:T(8,128)(2,1)S(1)}, u32[]{:S(2)}) copy-start(bf16[4,2,32,128]{3,2,1,0:T(8,128)(2,1)S(1)} %all-to-all-done.1.far_in) | copy-start | bytes 196612
  22.0 19.1 %all-to-all-start = ((bf16[8,3,32,128]{3,2,1,0:T(8,128)(2,1)}), bf16[8,3,32,128]{3,2,1,0:T(8,128)(2,1)S(1)}, u32[]{:S(2)}, u32[]{:S(2)}) async-start(bf16[8,3,32,128]{3,2,1,0:T(8,128)(2,1)} %get-tuple-element.14), calls=%async_computation | async-start | bytes 393216 | tf_op jit(solution)/shard_map/all_to_all | solution.py:240
  27.8 20.9 %collective-permute-start.3 = (f32[4,32,768]{2,1,0:T(8,128)S(1)}, f32[4,32,768]{2,1,0:T(8,128)}, u32[]{:S(2)}, u32[]{:S(2)}) collective-permute-start(f32[4,32,768]{2,1,0:T(8,128)S(1)} %get-tuple-element.35), channel_id=1, source_target_pairs={{1,0},{0,1},{3,2},{2,3},{5,4},{4,5},{7,6},{6,7},{9,8},{8,9},{11,10... | collective-permute-start | bytes 1179656 | tf_op jit(solution)/shard_map/ppermute | solution.py:192
  41.1 0.7 copy-start.8
  44.6 12.2 %all-to-all-start.3 = ((f32[4,32,768]{2,1,0:T(8,128)}), f32[4,32,768]{2,1,0:T(8,128)}, u32[]{:S(2)}, u32[]{:S(2)}) async-start(f32[4,32,768]{2,1,0:T(8,128)} %get-tuple-element.19), calls=%async_computation.3 | async-start | bytes 786432 | tf_op jit(solution)/shard_map/all_to_all | solution.py:278
  49.9 23.1 %collective-permute-start.4 = (f32[256,768]{1,0:T(8,128)S(1)}, f32[256,768]{1,0:T(8,128)}, u32[]{:S(2)}, u32[]{:S(2)}) collective-permute-start(f32[256,768]{1,0:T(8,128)S(1)} %bitcast.81), channel_id=1, source_target_pairs={{16,0},{24,8},{0,16},{8,24},{17,1},{25,9},{1,17},{9,25},{18,2},{26... | collective-permute-start | bytes 2359304 | tf_op jit(solution)/shard_map/ppermute | solution.py:192
  56.8 24.4 %all-to-all-start.2 = ((f32[8,32,768]{2,1,0:T(8,128)}), f32[8,32,768]{2,1,0:T(8,128)}, u32[]{:S(2)}, u32[]{:S(2)}) async-start(f32[8,32,768]{2,1,0:T(8,128)} %get-tuple-element.18), calls=%async_computation.2 | async-start | bytes 1572864 | tf_op jit(solution)/shard_map/all_to_all | solution.py:277
  76.1 12.0 %collective-permute-start.5 = (f32[2,256,768]{2,1,0:T(8,128)}, f32[2,256,768]{2,1,0:T(8,128)}, u32[]{:S(2)}, u32[]{:S(2)}) collective-permute-start(f32[2,256,768]{2,1,0:T(8,128)} %get-tuple-element.30), channel_id=1, source_target_pairs={{8,0},{0,8},{24,16},{16,24},{9,1},{1,9},{25,17},{17,25},{10,2},{2,... | collective-permute-start | bytes 4718600 | tf_op jit(solution)/shard_map/ppermute | solution.py:192
  83.4 23.9 %all-to-all-start.4 = ((f32[8,32,768]{2,1,0:T(8,128)}), f32[8,32,768]{2,1,0:T(8,128)S(1)}, u32[]{:S(2)}, u32[]{:S(2)}) async-start(f32[8,32,768]{2,1,0:T(8,128)} %broadcast_in_dim.76), calls=%async_computation.4 | async-start | bytes 1572864 | tf_op jit(solution)/shard_map/all_to_all | solution.py:281
  107.3 2.3 %copy-start.1 = (f32[2,2,256,768]{3,2,1,0:T(8,128)S(1)}, f32[2,2,256,768]{3,2,1,0:T(8,128)}, u32[]{:S(2)}) copy-start(f32[2,2,256,768]{3,2,1,0:T(8,128)} %pad_maximum_fusion) | copy-start | bytes 9437188
  109.6 4.6 %copy-start.3 = (f32[256,768]{1,0:T(8,128)}, f32[256,768]{1,0:T(8,128)S(1)}, u32[]{:S(2)}) copy-start(f32[256,768]{1,0:T(8,128)S(1)} %get-tuple-element.39) | copy-start | bytes 2359300
  122.2 1.8 copy-start.4
  124.0 5.3 %copy-start.2 = (f32[256,1024]{1,0:T(8,128)}, f32[256,1024]{1,0:T(8,128)S(1)}, u32[]{:S(2)}) copy-start(f32[256,1024]{1,0:T(8,128)S(1)} %fusion.13) | copy-start | bytes 3145732
  130.7 20.7 %collective-permute-start.8 = (f32[256,768]{1,0:T(8,128)}, f32[256,768]{1,0:T(8,128)}, u32[]{:S(2)}, u32[]{:S(2)}) collective-permute-start(f32[256,768]{1,0:T(8,128)} %fusion.18), channel_id=1, source_target_pairs={{16,0},{24,8},{0,16},{8,24},{17,1},{25,9},{1,17},{9,25},{18,2},{26... | collective-permute-start | bytes 2359304 | tf_op jit(solution)/shard_map/ppermute | solution.py:192
  132.6 34.5 %collective-permute-start.6 = (f32[256,768]{0,1:T(8,128)}, f32[256,768]{0,1:T(8,128)}, u32[]{:S(2)}, u32[]{:S(2)}) collective-permute-start(f32[256,768]{0,1:T(8,128)} %copy.21), channel_id=1, source_target_pairs={{16,0},{24,8},{0,16},{8,24},{17,1},{25,9},{1,17},{9,25},{18,2},{26... | collective-permute-start | bytes 2359304 | tf_op jit(solution)/shard_map/ppermute | solution.py:192
  151.4 15.7 %copy-start.6 = (f32[1,256,768]{1,2,0:T(8,128)S(1)}, f32[1,256,768]{1,2,0:T(8,128)}, u32[]{:S(2)}) copy-start(f32[1,256,768]{1,2,0:T(8,128)} %copy.22) | copy-start | bytes 2359300
  154.8 42.1 %collective-permute-start.9 = (f32[2,256,768]{2,1,0:T(8,128)}, f32[2,256,768]{2,1,0:T(8,128)}, u32[]{:S(2)}, u32[]{:S(2)}) collective-permute-start(f32[2,256,768]{2,1,0:T(8,128)} %get-tuple-element.28), channel_id=1, source_target_pairs={{8,0},{0,8},{24,16},{16,24},{9,1},{1,9},{25,17},{17,25},{10,2},{2,... | collective-permute-start | bytes 4718600 | tf_op jit(solution)/shard_map/ppermute | solution.py:192
  167.2 3.1 %copy-start.5 = (f32[256,768]{1,0:T(8,128)S(1)}, f32[256,768]{1,0:T(8,128)}, u32[]{:S(2)}) copy-start(f32[256,768]{1,0:T(8,128)} %copy-done.3) | copy-start | bytes 2359300
  170.2 26.6 %collective-permute-start.7 = (f32[2,256,768]{1,2,0:T(8,128)}, f32[2,256,768]{1,2,0:T(8,128)}, u32[]{:S(2)}, u32[]{:S(2)}) collective-permute-start(f32[2,256,768]{1,2,0:T(8,128)} %get-tuple-element.26), channel_id=1, source_target_pairs={{8,0},{0,8},{24,16},{16,24},{9,1},{1,9},{25,17},{17,25},{10,2},{2,... | collective-permute-start | bytes 4718600 | tf_op jit(solution)/shard_map/ppermute | solution.py:192
  171.9 24.0 %collective-permute-start.10 = (f32[32,768]{1,0:T(8,128)S(1)}, f32[32,768]{1,0:T(8,128)S(1)}, u32[]{:S(2)}, u32[]{:S(2)}) collective-permute-start(f32[32,768]{1,0:T(8,128)S(1)} %get-tuple-element.31), channel_id=1, source_target_pairs={{0,16},{8,24},{16,0},{24,8},{1,17},{9,25},{17,1},{25,9},{2,18},{10... | collective-permute-start | bytes 294920 | tf_op jit(solution)/shard_map/ppermute | solution.py:353
  172.7 23.2 %collective-permute-start.11 = (f32[32,768]{1,0:T(8,128)S(1)}, f32[32,768]{1,0:T(8,128)S(1)}, u32[]{:S(2)}, u32[]{:S(2)}) collective-permute-start(f32[32,768]{1,0:T(8,128)S(1)} %get-tuple-element.33), channel_id=1, source_target_pairs={{0,8},{8,0},{16,24},{24,16},{1,9},{9,1},{17,25},{25,17},{2,10},{10... | collective-permute-start | bytes 294920 | tf_op jit(solution)/shard_map/ppermute | solution.py:353
  173.0 23.0 %collective-permute-start.12 = (f32[32,768]{1,0:T(8,128)S(1)}, f32[32,768]{1,0:T(8,128)S(1)}, u32[]{:S(2)}, u32[]{:S(2)}) collective-permute-start(f32[32,768]{1,0:T(8,128)S(1)} %get-tuple-element.32), channel_id=1, source_target_pairs={{0,24},{8,16},{16,8},{24,0},{1,25},{9,17},{17,9},{25,1},{2,26},{10... | collective-permute-start | bytes 294920 | tf_op jit(solution)/shard_map/ppermute | solution.py:353

commit v2 on v1

v2 whole, which is shorter than its diff:
```python
import functools

import jax
import jax.numpy as jnp
from jax import lax
from jax.experimental import pallas as pl
from jax.experimental.pallas import tpu as pltpu
from jax.sharding import PartitionSpec as P

CAP = 2


SCALE = 1.0 / 0.07
EPS = 1e-06
ROOT_HALF = 0.7071067811865476
INV_ROOT_TWO_PI = 0.3989422804014327
VMEM_SPEC = pl.BlockSpec(memory_space=pltpu.VMEM)
SMEM_SPEC = pl.BlockSpec(memory_space=pltpu.SMEM)
PLAIN = (((1,), (0,)), ((), ()))
BY_LAST = (((1,), (1,)), ((), ()))
BY_FIRST = (((0,), (0,)), ((), ()))


def factors():
    groups = lax.axis_size("grp")
    inner = 2 if groups % 2 == 0 else 1
    return groups // inner, inner


def dev_factors():
    members = lax.axis_size("dev")
    outer = next(n for n in (4, 2, 1) if members % n == 0)
    return outer, members // outer


def place():
    members = lax.axis_size("dev")
    return lax.axis_index("grp"), lax.axis_index("dev"), members


def grp_at(grp, r):
    outer, inner = factors()
    return (grp // inner + r % outer) % outer * inner + (grp % inner + r // outer) % inner


def offset_of(grp, other):
    outer, inner = factors()
    return (other % inner - grp % inner + inner) % inner * outer + (
        other // inner - grp // inner + outer
    ) % outer


def negative(r):
    outer, inner = factors()
    return (-(r // outer)) % inner * outer + (-(r % outer)) % outer


def shift(value, axis, do, di, sizes):
    outer, inner = sizes
    pairs = [
        (((o + do) % outer) * inner + (i + di) % inner, o * inner + i)
        for o in range(outer)
        for i in range(inner)
    ]
    return lax.ppermute(value, axis, pairs)


def shift_grp(value, r):
    outer, _ = factors()
    return shift(value, "grp", r % outer, r // outer, factors())


def call(kernel, flops, outs, ins, scratch=(), aliases=None):
    specs = [SMEM_SPEC if scalar else VMEM_SPEC for _, scalar in ins]
    out_shape = tuple(jax.ShapeDtypeStruct(s, d) for s, d in outs)
    out_specs = tuple(
        SMEM_SPEC if len(s) == 1 and d == jnp.int32 else VMEM_SPEC for s, d in outs
    )
    moved = sum(x.size * x.dtype.itemsize for x, _ in ins)
    return pl.pallas_call(
        kernel,
        out_shape=out_shape,
        in_specs=specs,
        out_specs=out_specs,
        scratch_shapes=list(scratch),
        input_output_aliases=aliases or {},
        cost_estimate=pl.CostEstimate(
            flops=int(flops), bytes_accessed=int(moved), transcendentals=0
        ),
    )(*[x for x, _ in ins])


def split(value):
    high = value.astype(jnp.bfloat16)
    return high, (value - high.astype(jnp.float32)).astype(jnp.bfloat16)


def dot3(a, b, dims):
    one = functools.partial(
        lax.dot_general, dimension_numbers=dims, preferred_element_type=jnp.float32
    )
    return one(a[0], b[0]) + (one(a[0], b[1]) + one(a[1], b[0]))


def pick_kernel(blocks_dev, lists, sel, pair, tiles, near, far, rows, selm, count):
    grp, dev, members = place()
    device = grp * members + dev
    tile_dev, block_rows, _ = tiles.shape
    sel_dev = selm.shape[0]
    base = device * blocks_dev * block_rows
    lane = lax.broadcasted_iota(jnp.int32, (1, block_rows), 1)
    coded = jnp.zeros((1, block_rows), jnp.int32)
    for k in range(sel_dev):
        selm[k : k + 1, :] = (sel[k] - base) - lane
        coded = jnp.where(lane == k, pair[k], coded)
    near[...] = jnp.zeros_like(near)
    far[...] = jnp.zeros_like(far)
    for i in range(count.shape[0]):
        count[i] = 0
    offsets = selm[...]
    for t in range(tile_dev):
        row_block = lists[0, device * tile_dev + t] - device * blocks_dev
        hot = (offsets == row_block * block_rows).astype(jnp.bfloat16)
        rows[t] = jnp.dot(hot, tiles[t], preferred_element_type=jnp.float32).astype(jnp.bfloat16)
    high = coded // block_rows
    high_row = high.astype(jnp.float32).astype(jnp.bfloat16)
    low_row = (coded - high * block_rows).astype(jnp.float32).astype(jnp.bfloat16)
    for q in range(near.shape[0]):
        near[q, CAP, 0:1, :] = high_row
        near[q, CAP, 1:2, :] = low_row

    def step(t, carry):
        owner = lists[1, device * tile_dev + t] // blocks_dev
        rank = count[owner]
        count[owner] = rank + 1
        owner_grp = owner // members
        owner_dev = owner - owner_grp * members

        @pl.when((owner_grp == grp) & (owner_dev != dev))
        def _():
            near[owner_dev, rank] = rows[t]

        @pl.when(owner_grp != grp)
        def _():
            far[offset_of(grp, owner_grp), rank] = rows[t]

        return carry

    lax.fori_loop(0, tile_dev, step, 0)


def index_kernel(lists, sel, feats, blocks, own_feats, index):
    grp, dev, members = place()
    groups = lax.axis_size("grp")
    device = grp * members + dev
    blocks_dev, block_rows, _ = blocks.shape
    tile_dev = lists.shape[1] // (groups * members)
    sel_dev = own_feats.shape[0]
    base = device * blocks_dev * block_rows
    for c in range(blocks_dev):
        blocks[c] = feats[c * block_rows : (c + 1) * block_rows, :].astype(jnp.bfloat16)
    for k in range(sel_dev):
        own_feats[k : k + 1, :] = feats[pl.ds(sel[k] - base, 1), :]
    for i in range(index.shape[0]):
        index[i] = 0
    for q in range(members + groups):
        peer = grp * members + q if q < members else grp_at(grp, negative(q - members)) * members + dev

        def scan(t, hits, q=q, peer=peer):
            column = lists[1, peer * tile_dev + t]
            mine = column // blocks_dev == device
            index[q * (CAP + 1) + hits] = jnp.clip(column - device * blocks_dev, 0, blocks_dev - 1)
            return jnp.minimum(hits + mine.astype(jnp.int32), CAP)

        lax.fori_loop(0, tile_dev, scan, 0, unroll=4)


def partial_kernel(first, index, rows_in, blocks, part):
    for p in range(part.shape[0]):
        at = (first + p) * (CAP + 1)
        total = jnp.dot(rows_in[p, 0], blocks[index[at]], preferred_element_type=jnp.float32)
        for s in range(1, CAP):
            total += jnp.dot(
                rows_in[p, s], blocks[index[at + s]], preferred_element_type=jnp.float32
            )
        part[p] = total


def local_kernel(lists, own_feats, rows, blocks, local):
    grp, dev, members = place()
    device = grp * members + dev
    blocks_dev = blocks.shape[0]
    tile_dev = rows.shape[0]
    local[...] = own_feats[...]

    def add_tile(t, carry):
        column = lists[1, device * tile_dev + t]

        @pl.when(column // blocks_dev == device)
        def _():
            local[...] += jnp.dot(
                rows[t], blocks[column - device * blocks_dev], preferred_element_type=jnp.float32
            )

        return carry

    lax.fori_loop(0, tile_dev, add_tile, 0)


def combine_kernel(near_back, local, *rest):
    total = local[...]
    for p in range(near_back.shape[0]):
        total += near_back[p]
    for part in rest[:-1]:
        total += part[...]
    out = rest[-1]
    for p in range(out.shape[0]):
        out[p] = total


def split_kernel(value, high, mid):
    high[...], mid[...] = split(value[...])


def texts_kernel(*refs):
    pieces, (high, mid) = refs[:-2], refs[-2:]
    for r, piece in enumerate(pieces):
        rows = piece[...]
        norm = jnp.sqrt(jnp.sum(rows * rows, axis=1, keepdims=True) + EPS)
        high[r], mid[r] = split(rows / norm)


def forward_kernel(
    chosen, w_high, w_mid, t_high, t_mid, pair, ids, unit, slope, exps, row_total, sums
):
    grp, _, _ = place()
    groups = t_high.shape[0]
    before = dot3(split(chosen[...]), (w_high[...], w_mid[...]), PLAIN)
    bell = 0.5 * (1.0 + lax.erf(before * ROOT_HALF))
    hidden = before * bell
    norm = jnp.sqrt(jnp.sum(hidden * hidden, axis=1, keepdims=True) + EPS)
    nodes = hidden / norm
    unit[...] = nodes
    slope[...] = (bell + before * jnp.exp(-0.5 * before * before) * INV_ROOT_TWO_PI) / norm
    parts = split(nodes)
    rows = jnp.zeros((nodes.shape[0], 1), jnp.float32)
    positive = jnp.zeros((nodes.shape[0], 1), jnp.float32)
    for r in range(groups):
        scores = SCALE * dot3(parts, (t_high[r], t_mid[r]), BY_LAST)
        hit = pair[...] == ids[r]
        positive += jnp.sum(jnp.where(hit, scores, 0.0), axis=1, keepdims=True)
        grown = jnp.exp(scores)
        exps[r] = grown
        rows += jnp.sum(grown, axis=1, keepdims=True)
        sums[pl.ds(grp_at(grp, r), 1), :] = jnp.sum(grown, axis=0, keepdims=True)
    row_total[...] = rows
    lane = lax.broadcasted_iota(jnp.int32, (1, sums.shape[1]), 1)
    logs = jnp.sum(jnp.log(rows), axis=0, keepdims=True)
    found = jnp.sum(positive, axis=0, keepdims=True)
    sums[groups : groups + 1, :] = jnp.where(lane == 0, logs, jnp.where(lane == 1, found, 0.0))


def backward_kernel(
    exps, row_total, totals, pair, ids, t_high, t_mid, unit, slope, pre_grad, own_cols, loss
):
    grp, _, _ = place()
    groups = t_high.shape[0]
    sel_dev = own_cols.shape[2]
    row_share = 0.5 / row_total[...]
    node_dir = jnp.zeros(pre_grad.shape, jnp.float32)
    for r in range(groups):
        col_share = 0.5 / totals[pl.ds(grp_at(grp, r), 1), :]
        hit = (pair[...] == ids[r]).astype(jnp.float32)
        grads = exps[r] * (row_share + col_share) - hit
        own_cols[r] = grads[:, :sel_dev]
        node_dir += dot3(split(grads), (t_high[r], t_mid[r]), PLAIN)
    node_dir = SCALE * node_dir
    nodes = unit[...]
    along = jnp.sum(nodes * node_dir, axis=1, keepdims=True)
    pre_grad[...] = (node_dir - nodes * along) * slope[...]
    all_sel = groups * totals.shape[1]
    logs = totals[groups : groups + 1, 0:1] + jnp.sum(
        jnp.sum(jnp.log(totals[0:groups, :]), axis=1, keepdims=True), axis=0, keepdims=True
    )
    loss[...] = logs / (2.0 * all_sel) - totals[groups : groups + 1, 1:2] / all_sel


def rows_kernel(pre_grad, w_high, w_mid, near_grads, own_grads, own_half):
    _, dev, members = place()
    sel_dev = own_grads.shape[0]
    grads = dot3(split(pre_grad[...]), (w_high[...], w_mid[...]), BY_LAST)
    for q in range(members):
        part = grads[q * sel_dev : (q + 1) * sel_dev, :]
        near_grads[q] = part.astype(jnp.bfloat16)

        @pl.when(dev == q)
        def _(part=part):
            own_grads[...] = part
            own_half[...] = part.astype(jnp.bfloat16)


def text_part_kernel(own_cols, unit, part):
    parts = split(unit[...])
    for r in range(part.shape[0]):
        part[r] = SCALE * dot3(split(own_cols[r]), parts, BY_FIRST)


def text_end_kernel(texts, *rest):
    parts, out = rest[:-1], rest[-1]
    rows = texts[...]
    norm = jnp.sqrt(jnp.sum(rows * rows, axis=1, keepdims=True) + EPS)
    unit = rows / norm
    total = parts[0][...]
    for part in parts[1:]:
        total += part[...]
    out[...] = (total - unit * jnp.sum(unit * total, axis=1, keepdims=True)) / norm


def spread_kernel(lists, sel, index, near_in, rows, near_grads, own_grads, out):
    grp, dev, members = place()
    device = grp * members + dev
    tile_dev, sel_dev, block_rows = rows.shape
    blocks_dev = out.shape[0] // block_rows
    base = device * blocks_dev * block_rows
    out[...] = jnp.zeros_like(out)
    for q in range(members):
        for s in range(CAP):
            c = index[q * (CAP + 1) + s]
            span = pl.ds(pl.multiple_of(c * block_rows, block_rows), block_rows)
            out[span, :] += lax.dot_general(
                near_in[q, s], near_grads[q], BY_FIRST, preferred_element_type=jnp.float32
            )
    own = near_grads[dev]

    def add_tile(t, carry):
        column = lists[1, device * tile_dev + t]

        @pl.when(column // blocks_dev == device)
        def _():
            c = column - device * blocks_dev
            span = pl.ds(pl.multiple_of(c * block_rows, block_rows), block_rows)
            out[span, :] += lax.dot_general(
                rows[t], own, BY_FIRST, preferred_element_type=jnp.float32
            )

        return carry

    lax.fori_loop(0, tile_dev, add_tile, 0)
    for k in range(sel_dev):
        out[pl.ds(sel[k] - base, 1), :] += own_grads[k : k + 1, :]


def spread_far_kernel(first, index, so_far, *refs):
    out = refs[-1]
    count = (len(refs) - 1) // 2
    rows_in, grads = refs[:count], refs[count : 2 * count]
    block_rows = rows_in[0].shape[2]
    out[...] = so_far[...]
    for p in range(count):
        for s in range(CAP):
            c = index[(first + p) * (CAP + 1) + s]
            span = pl.ds(pl.multiple_of(c * block_rows, block_rows), block_rows)
            out[span, :] += lax.dot_general(
                rows_in[p][s], grads[p][...], BY_FIRST, preferred_element_type=jnp.float32
            )


def weight_kernel(*refs):
    out = refs[-1]
    rest = refs[:-1]
    total = None
    if len(rest) % 2:
        total, rest = rest[0][...], rest[1:]
    for i in range(0, len(rest), 2):
        term = dot3(split(rest[i][...]), split(rest[i + 1][...]), BY_FIRST)
        total = term if total is None else total + term
    out[...] = total


def shards(node_features, tiles, tile_list, weight, texts, selected, pairing):
    groups = lax.axis_size("grp")
    members = lax.axis_size("dev")
    grp_index = lax.axis_index("grp")
    dev_index = lax.axis_index("dev")
    block_rows = tiles.shape[1]
    width = node_features.shape[1]
    blocks_dev = node_features.shape[0] // block_rows
    tile_dev = tiles.shape[0]
    sel_dev = selected.shape[0]
    group_sel = sel_dev * members
    f32, half = jnp.float32, jnp.bfloat16
    outer, inner = factors()
    dev_outer, dev_inner = dev_factors()
    lists = tile_list.T
    dots = 2 * 3 * group_sel * width

    text_z = [texts] + [shift(texts, "dev", j, 0, dev_factors()) for j in range(1, dev_outer)]

    near_rows, far_rows, tile_rows = call(
        functools.partial(pick_kernel, blocks_dev),
        2 * tile_dev * sel_dev * block_rows * block_rows,
        [
            ((members, CAP + 1, sel_dev, block_rows), half),
            ((groups, CAP, sel_dev, block_rows), half),
            ((tile_dev, sel_dev, block_rows), half),
        ],
        [(lists, True), (selected, True), (pairing, True), (tiles, False)],
        [
            pltpu.VMEM((sel_dev, block_rows), jnp.int32),
            pltpu.SMEM((groups * members,), jnp.int32),
        ],
    )
    near_in = lax.all_to_all(near_rows, "dev", 0, 0, tiled=True)
    far_in = [shift_grp(far_rows[r], negative(r)) for r in range(1, groups)]

    blocks, own_feats, index = call(
        index_kernel,
        10**7,
        [
            ((blocks_dev, block_rows, width), half),
            ((sel_dev, width), f32),
            (((members + groups) * (CAP + 1),), jnp.int32),
        ],
        [(lists, True), (selected, True), (node_features, False)],
    )
    (near_part,) = call(
        functools.partial(partial_kernel, 0),
        2 * members * CAP * sel_dev * block_rows * width,
        [((members, sel_dev, width), f32)],
        [(index, True), (near_in, False), (blocks, False)],
    )
    near_back = lax.all_to_all(near_part, "dev", 0, 0, tiled=True)
    (far_part,) = call(
        functools.partial(partial_kernel, members + 1),
        2 * groups * CAP * sel_dev * block_rows * width,
        [((groups - 1, sel_dev, width), f32)],
        [(index, True), (jnp.stack(far_in), False), (blocks, False)],
    )
    far_back = [shift_grp(far_part[r - 1], r) for r in range(1, groups)]
    (local,) = call(
        local_kernel,
        2 * tile_dev * sel_dev * block_rows * width,
        [((sel_dev, width), f32)],
        [(lists, True), (own_feats, False), (tile_rows, False), (blocks, False)],
    )

    text_near = jnp.concatenate(text_z, axis=0)
    text_near = jnp.concatenate(
        [text_near] + [shift(text_near, "dev", 0, j, dev_factors()) for j in range(1, dev_inner)],
        axis=0,
    )
    text_pieces = gather_grp(text_near)
    t_high, t_mid = call(
        texts_kernel,
        10**8,
        [((groups, group_sel, width), half)] * 2,
        [(piece, False) for piece in text_pieces],
    )
    w_high, w_mid = call(split_kernel, 10**7, [((width, width), half)] * 2, [(weight, False)])
    dev_o = (dev_index // dev_inner + jnp.arange(dev_outer, dtype=jnp.int32)) % dev_outer
    dev_i = (dev_index % dev_inner + jnp.arange(dev_inner, dtype=jnp.int32)) % dev_inner
    dev_of = (dev_o[None, :] * dev_inner + dev_i[:, None]).reshape(-1)
    grp_of = grp_at(grp_index, jnp.arange(groups, dtype=jnp.int32))
    ids = (
        (grp_of[:, None, None] * members + dev_of[None, :, None]) * sel_dev
        + jnp.arange(sel_dev, dtype=jnp.int32)[None, None, :]
    ).reshape(groups, 1, group_sel)
    coded = near_in[:, CAP, :2, :sel_dev].astype(jnp.int32)
    pair = (coded[:, 0, :] * block_rows + coded[:, 1, :]).reshape(group_sel, 1)

    (copies,) = call(
        combine_kernel,
        10**6,
        [((members, sel_dev, width), f32)],
        [(near_back, False), (local, False)] + [(part, False) for part in far_back],
    )
    chosen = lax.all_to_all(copies, "dev", 0, 0, tiled=True).reshape(group_sel, width)
    chosen_pieces = gather_grp(chosen)

    unit, slope, exps, row_total, sums = call(
        forward_kernel,
        dots * (width + groups * group_sel),
        [
            ((group_sel, width), f32),
            ((group_sel, width), f32),
            ((groups, group_sel, group_sel), f32),
            ((group_sel, 1), f32),
            ((groups + 1, group_sel), f32),
        ],
        [(x, False) for x in (chosen, w_high, w_mid, t_high, t_mid, pair, ids)],
    )
    totals = lax.psum(sums, "grp")
    pre_grad, own_cols, loss = call(
        backward_kernel,
        dots * groups * group_sel,
        [
            ((group_sel, width), f32),
            ((groups, group_sel, sel_dev), f32),
            ((1, 1), f32),
        ],
        [(x, False) for x in (exps, row_total, totals, pair, ids, t_high, t_mid, unit, slope)],
    )
    pre_pieces = gather_grp(pre_grad)
    near_grads, own_grads, own_half = call(
        rows_kernel,
        dots * width,
        [((members, sel_dev, width), half), ((sel_dev, width), f32), ((sel_dev, width), half)],
        [(x, False) for x in (pre_grad, w_high, w_mid)],
    )
    far_grads = gather_grp(own_half)
    (text_part,) = call(
        text_part_kernel,
        2 * 3 * groups * sel_dev * group_sel * width,
        [((groups, sel_dev, width), f32)],
        [(own_cols, False), (unit, False)],
    )
    text_part = text_part.reshape(inner, outer, sel_dev, width)
    text_sum = text_part[0]
    for j in range(1, inner):
        text_sum = text_sum + shift_grp(text_part[j], negative(j * outer))
    text_terms = [text_sum[0]] + [
        shift_grp(text_sum[j], negative(j)) for j in range(1, outer)
    ]
    (grad_texts,) = call(
        text_end_kernel,
        10**6,
        [((sel_dev, width), f32)],
        [(texts, False)] + [(term, False) for term in text_terms],
    )
    (spread,) = call(
        spread_kernel,
        4 * tile_dev * sel_dev * block_rows * width,
        [(node_features.shape, f32)],
        [(x, True) for x in (lists, selected, index)]
        + [(x, False) for x in (near_in, tile_rows, near_grads, own_grads)],
    )
    (grad_nodes,) = call(
        functools.partial(spread_far_kernel, members + 1),
        4 * tile_dev * sel_dev * block_rows * width,
        [(node_features.shape, f32)],
        [(index, True), (spread, False)]
        + [(x, False) for x in far_in]
        + [(far_grads[negative(r)], False) for r in range(1, groups)],
        aliases={1: 0},
    )

    order = sorted(range(groups), key=lambda r: (r % outer > 0, r))
    grad_weight = None
    for r in order:
        ins = [(chosen_pieces[r], False), (pre_pieces[r], False)]
        first = [] if grad_weight is None else [(grad_weight, False)]
        (grad_weight,) = call(
            weight_kernel,
            dots * width,
            [((width, width), f32)],
            first + ins,
            aliases={0: 0} if first else None,
        )
    return (loss.reshape(()), grad_nodes, grad_weight, grad_texts)


def gather_grp(part):
    outer, inner = factors()
    pieces = [part] + [shift_grp(part, j) for j in range(1, outer)]
    return pieces + [shift_grp(p, j * outer) for j in range(1, inner) for p in pieces]


def solution(mesh):
    return jax.shard_map(
        shards,
        mesh=mesh,
        in_specs=(
            P(("grp", "dev"), None),
            P(("grp", "dev"), None, None),
            P(),
            P(),
            P(("grp", "dev"), None),
            P(("grp", "dev")),
            P(("grp", "dev")),
        ),
        out_specs=(P(), P(("grp", "dev"), None), P(), P(("grp", "dev"), None)),
        check_vma=False,
    )
```

time: 213 us -> 195 us (0.915)
  Pallas kernels: 25 us -> 78 us
  matrix products: 31.4 us -> 0 us
  other arithmetic: 28.3 us -> 3.12 us
  waiting for transfers between devices: 65.3 us -> 59.9 us
  blocking collectives: 12.2 us -> 7.24 us
  between operations: 4.02 us -> 0.85 us
    pallas_call x4 -> x19, Pallas kernels: 25 us -> 78 us  [call(): pl.pallas_call(kernel, out_shape=out_shape, in_specs=specs, out_specs=out...]
    dot_general x6 -> x0, matrix products: 31.4 us -> none  [the longest x1 13.5 us: shards(): lax.dot_general(chosen_all, pre_all, (((0,), (0,)), ((), ())), precision=...]
    all_to_all x3 -> x1, waiting for transfers between devices: 24.2 us -> 9.28 us  [shards(): lax.all_to_all(copies, 'dev', 0, 0, tiled=True).reshape(group_sel, width)]
    another operation x7 -> x1, other arithmetic: 15.4 us -> 0.63 us  [shards(): jnp.stack(far_in)]
    ppermute x10 -> x24, waiting for transfers between devices: 37.4 us -> 50.6 us  [shift(): return lax.ppermute(value, axis, pairs)]
    ppermute x10 -> x24, starting transfers between devices: 12.2 us -> 19.1 us  [shift(): return lax.ppermute(value, axis, pairs)]
    all_gather x1 -> x0, blocking collectives: 6.26 us -> none  [shards(): far_grads = lax.all_gather(own_grads.astype(jnp.bfloat16), 'grp', axis=0)]
    all_to_all x3 -> x1, starting transfers between devices: 10.9 us -> 4.82 us  [shards(): lax.all_to_all(copies, 'dev', 0, 0, tiled=True).reshape(group_sel, width)]
  transfers between devices with their start and end apart: 18 -> 27, of which waited for: 7 -> 8; matrix products, arithmetic and copies ran while one was open for 17% -> 3% of each run, Pallas kernels for 12% -> 30%
where the time goes in v2:
time: 195 us; the launch traced here: 194 us
  Pallas kernels  78 us (40%)
  waiting for transfers between devices  59.9 us (31%)
  starting transfers between devices  36.1 us (19%)
  local copies, waits for them, and re-layouts  9.14 us (5%)
  blocking collectives  7.24 us (4%)
  other arithmetic  3.12 us (2%)
    pallas_call x19, Pallas kernels, call(): pl.pallas_call(kernel, out_shape=out_shape, in_specs=specs, out_specs=out...  78 us
    ppermute x24, waiting for transfers between devices, shift(): return lax.ppermute(value, axis, pairs)  50.6 us
    ppermute x24, starting transfers between devices, shift(): return lax.ppermute(value, axis, pairs)  19.1 us
    all_to_all x1, waiting for transfers between devices, shards(): lax.all_to_all(copies, 'dev', 0, 0, tiled=True).reshape(group_sel, width)  9.28 us
    all_to_all x1, starting transfers between devices, shards(): near_in = lax.all_to_all(near_rows, 'dev', 0, 0, tiled=True)  7.31 us
    psum x1, blocking collectives, shards(): totals = lax.psum(sums, 'grp')  7.24 us
    unnamed x50, local copies, waits for them, and re-layouts  5.63 us
    all_to_all x1, starting transfers between devices, shards(): near_back = lax.all_to_all(near_part, 'dev', 0, 0, tiled=True)  4.88 us
  transfers between devices with their start and end apart: 27, of which 8 were waited for; matrix products, arithmetic and copies ran while one was open for 3% of the time, Pallas kernels for 30%

profile of v2, /device:TPU:0, one launch (start us, length us, event | category | flops | bytes accessed | tf_op | source)
XLA Modules:
  0.0 194.3 jit_solution(17671388326778222434)
XLA Ops:
  0.6 3.4 %shard_map.103 = (bf16[8,3,32,128]{3,2,1,0:T(8,128)(2,1)}, bf16[4,2,32,128]{3,2,1,0:T(8,128)(2,1)}, bf16[28,32,128]{2,1,0:T(8,128)(2,1)}) custom-call(s32[2,896]{1,0:T(2,128)} %bitcast.31, s32[32]{0:T(128)} %sel.5, s32[32]{0:T(128)} %pair.1, bf16[28,128,128]{2,1,0:T(8,128)(2,1)} %tiles.1), custom_call_target="tpu_custom_call" | custom-call | flops 29360128 | bytes 924928 | tf_op jit(solution)/shard_map/pallas_call | solution.py:80
  4.0 7.3 %all-to-all-start = ((bf16[8,3,32,128]{3,2,1,0:T(8,128)(2,1)}), bf16[8,3,32,128]{3,2,1,0:T(8,128)(2,1)S(1)}, u32[]{:S(2)}, u32[]{:S(2)}) async-start(bf16[8,3,32,128]{3,2,1,0:T(8,128)(2,1)} %get-tuple-element.26), calls=%async_computation | async-start | bytes 393216 | tf_op jit(solution)/shard_map/all_to_all | solution.py:413
  11.3 3.8 %collective-permute-start.6 = (f32[32,768]{1,0:T(8,128)}, f32[32,768]{1,0:T(8,128)S(1)}, u32[]{:S(2)}, u32[]{:S(2)}) collective-permute-start(f32[32,768]{1,0:T(8,128)} %texts.1), channel_id=1, source_target_pairs={{2,0},{3,1},{4,2},{5,3},{6,4},{7,5},{0,6},{1,7},{10,8},{11,9},{12,... | collective-permute-start | bytes 294920 | tf_op jit(solution)/shard_map/ppermute | solution.py:65
  16.3 6.3 %shard_map.102 = (bf16[4,128,768]{2,1,0:T(8,128)(2,1)}, f32[32,768]{1,0:T(8,128)}, s32[36]{0:T(128)}) custom-call(s32[2,896]{1,0:T(2,128)} %bitcast.32, s32[32]{0:T(128)} %sel.5, f32[512,768]{1,0:T(8,128)} %feats.1), custom_call_target="tpu_custom_call" | custom-call | flops 10000000 | bytes 1580160 | tf_op jit(solution)/shard_map/pallas_call | solution.py:80
  23.3 2.7 %shard_map.104 = f32[8,32,768]{2,1,0:T(8,128)} custom-call(s32[36]{0:T(128)} %get-tuple-element.25.index, bf16[8,3,32,128]{3,2,1,0:T(8,128)(2,1)} %copy-done.3, bf16[4,128,768]{2,1,0:T(8,128)(2,1)} %get-tuple-element.27.blocks), custom_call_target="tpu_custom_call" | custom-call | flops 100663296 | bytes 983184 | tf_op jit(solution)/shard_map/pallas_call | solution.py:80
  26.0 4.9 %all-to-all-start.1 = ((f32[8,32,768]{2,1,0:T(8,128)}), f32[8,32,768]{2,1,0:T(8,128)S(1)}, u32[]{:S(2)}, u32[]{:S(2)}) async-start(f32[8,32,768]{2,1,0:T(8,128)} %shard_map.104), calls=%async_computation.1 | async-start | bytes 1572864 | tf_op jit(solution)/shard_map/all_to_all | solution.py:432
  33.2 2.1 %collective-permute-start.9 = (f32[128,768]{1,0:T(8,128)S(1)}, f32[128,768]{1,0:T(8,128)S(1)}, u32[]{:S(2)}, u32[]{:S(2)}) collective-permute-start(f32[128,768]{1,0:T(8,128)S(1)} %pad_maximum_fusion), channel_id=1, source_target_pairs={{1,0},{0,1},{3,2},{2,3},{5,4},{4,5},{7,6},{6,7},{9,8},{8,9},{11,10... | collective-permute-start | bytes 1179656 | tf_op jit(solution)/shard_map/ppermute | solution.py:65
  36.3 2.2 %shard_map.106 = f32[3,32,768]{2,1,0:T(8,128)} custom-call(s32[36]{0:T(128)} %get-tuple-element.25.index, bf16[3,2,32,128]{3,2,1,0:T(8,128)(2,1)} %pad_maximum_fusion.1.rows_in, bf16[4,128,768]{2,1,0:T(8,128)(2,1)} %get-tuple-element.27.blocks), custom_call_target="tpu_custom_call" | custom-call | flops 50331648 | bytes 835728 | tf_op jit(solution)/shard_map/pallas_call | solution.py:80
  38.6 11.2 %collective-permute-done.9 = f32[128,768]{1,0:T(8,128)S(1)} collective-permute-done((f32[128,768]{1,0:T(8,128)S(1)}, f32[128,768]{1,0:T(8,128)S(1)}, u32[]{:S(2)}, u32[]{:S(2)}) %collective-permute-start.9) | collective-permute-done | bytes 393248 | tf_op jit(solution)/shard_map/ppermute | solution.py:65
  49.8 1.6 collective-permute-start.10
  52.0 1.6 collective-permute-start.5
  53.7 4.4 %shard_map.105.local = f32[32,768]{1,0:T(8,128)} custom-call(s32[2,896]{1,0:T(2,128)} %bitcast.33, f32[32,768]{1,0:T(8,128)} %get-tuple-element.28.own_feats, bf16[28,32,128]{2,1,0:T(8,128)(2,1)} %get-tuple-element.29.rows, bf16[4,128,768]{2,1,0:T(8,128)(2,1)} %get-tuple-element.27.blocks), custom_call_target="tpu_custom_call" | custom-call | flops 176160768 | bytes 1121280 | tf_op jit(solution)/shard_map/pallas_call | solution.py:80
  58.1 13.8 %collective-permute-done.3.rest_0_ = f32[32,768]{1,0:T(8,128)S(1)} collective-permute-done((f32[32,768]{1,0:T(8,128)S(1)}, f32[32,768]{1,0:T(8,128)S(1)}, u32[]{:S(2)}, u32[]{:S(2)}) %collective-permute-start.3) | collective-permute-done | bytes 98336 | tf_op jit(solution)/shard_map/ppermute | solution.py:65
  73.5 2.2 %shard_map.107 = f32[8,32,768]{2,1,0:T(8,128)} custom-call(f32[8,32,768]{2,1,0:T(8,128)} %copy-done, f32[32,768]{1,0:T(8,128)} %shard_map.105.local, f32[32,768]{1,0:T(8,128)} %copy-done.14, f32[32,768]{1,0:T(8,128)} %copy-done.15, f32[32,768]{1,0:T(8,128)} %copy-done.16), custom_call_target="tpu_custom_call" | custom-call | flops 1000000 | bytes 1179648 | tf_op jit(solution)/shard_map/pallas_call | solution.py:80
  75.7 4.8 %all-to-all-start.2 = ((f32[8,32,768]{2,1,0:T(8,128)}), f32[8,32,768]{2,1,0:T(8,128)S(1)}, u32[]{:S(2)}, u32[]{:S(2)}) async-start(f32[8,32,768]{2,1,0:T(8,128)} %shard_map.107), calls=%async_computation.2 | async-start | bytes 1572864 | tf_op jit(solution)/shard_map/all_to_all | solution.py:477
  81.7 3.2 %shard_map.108 = (bf16[768,768]{1,0:T(8,128)(2,1)}, bf16[768,768]{1,0:T(8,128)(2,1)}) custom-call(f32[768,768]{1,0:T(8,128)} %value.1), custom_call_target="tpu_custom_call" | custom-call | flops 10000000 | bytes 2359296 | tf_op jit(solution)/shard_map/pallas_call | solution.py:80
  88.0 4.4 %shard_map.109 = (bf16[4,256,768]{2,1,0:T(8,128)(2,1)}, bf16[4,256,768]{2,1,0:T(8,128)(2,1)}) custom-call(f32[256,768]{1,0:T(8,128)} %copy-done.6, f32[256,768]{1,0:T(8,128)} %copy-done.11, f32[256,768]{1,0:T(8,128)} %copy-done.12, f32[256,768]{1,0:T(8,128)} %collective-permute-done.12.refs_3_), custom_call_target="tpu_custom_call" | custom-call | flops 100000000 | bytes 3145728 | tf_op jit(solution)/shard_map/pallas_call | solution.py:80
  92.4 9.3 %all-to-all-done.2 = f32[8,32,768]{2,1,0:T(8,128)S(1)} async-done(((f32[8,32,768]{2,1,0:T(8,128)}), f32[8,32,768]{2,1,0:T(8,128)S(1)}, u32[]{:S(2)}, u32[]{:S(2)}) %all-to-all-start.2) | async-done | bytes 786464 | tf_op jit(solution)/shard_map/all_to_all | solution.py:477
  102.5 6.7 %shard_map.110 = (f32[256,768]{1,0:T(8,128)}, f32[256,768]{1,0:T(8,128)}, f32[4,256,256]{2,1,0:T(8,128)}, f32[256,1]{1,0:T(8,128)}, f32[5,256]{1,0:T(8,128)}) custom-call(f32[256,768]{1,0:T(8,128)} %bitcast.27, bf16[768,768]{1,0:T(8,128)(2,1)} %get-tuple-element.31.w_high, bf16[768,768]{1,0:T(8,128)(2,1)} %get-tuple-element.32.w_mid, ...), custom_call_target="tpu_custom_call" | custom-call | flops 2113929216 | bytes 6296576 | tf_op jit(solution)/shard_map/pallas_call | solution.py:80
  109.2 7.2 %psum.7.totals = f32[5,256]{1,0:T(8,128)} all-reduce(f32[5,256]{1,0:T(8,128)} %get-tuple-element.37), channel_id=1, replica_groups=mesh['grp'=4,'dev'=8] {'grp'}, use_global_device_ids=true, to_apply=%region_0.1 | all-reduce | flops 1280 | bytes 10240 | tf_op jit(solution)/shard_map/psum | solution.py:492
  116.5 5.4 %shard_map.111 = (f32[256,768]{1,0:T(8,128)}, f32[4,256,32]{2,1,0:T(8,128)}, f32[1,1]{1,0:T(1,128)}) custom-call(f32[4,256,256]{2,1,0:T(8,128)} %get-tuple-element.35.exps, f32[256,1]{1,0:T(8,128)} %get-tuple-element.36.row_total, f32[5,256]{1,0:T(8,128)} %psum.7.totals, s32[256,1]{1,0:T(8,128)} %add.219.pair, s32[4,1,256]{2,1,0:T(1,128)} %broadcast_add_fusion.ids, ...), custom_call_target="tpu_custom_call" | custom-call | flops 1207959552 | bytes 5778432 | tf_op jit(solution)/shard_map/pallas_call | solution.py:80
  123.9 4.0 %shard_map.112 = (bf16[8,32,768]{2,1,0:T(8,128)(2,1)}, f32[32,768]{1,0:T(8,128)}, bf16[32,768]{1,0:T(8,128)(2,1)}) custom-call(f32[256,768]{1,0:T(8,128)} %get-tuple-element.41.pre_grad.refs_1_, bf16[768,768]{1,0:T(8,128)(2,1)} %get-tuple-element.31.w_high, bf16[768,768]{1,0:T(8,128)(2,1)} %get-tuple-element.32.w_mid), custom_call_target="tpu_custom_call" | custom-call | flops 905969664 | bytes 3145728 | tf_op jit(solution)/shard_map/pallas_call | solution.py:80
  129.3 3.0 %shard_map.119 = f32[4,32,768]{2,1,0:T(8,128)} custom-call(f32[4,256,32]{2,1,0:T(8,128)} %get-tuple-element.45.own_cols, f32[256,768]{1,0:T(8,128)} %get-tuple-element.38.unit), custom_call_target="tpu_custom_call" | custom-call | flops 150994944 | bytes 917504 | tf_op jit(solution)/shard_map/pallas_call | solution.py:80
  132.3 1.7 slice.61
  134.0 24.5 %collective-permute-done.13.refs_3_ = bf16[32,768]{1,0:T(8,128)(2,1)} collective-permute-done((bf16[32,768]{1,0:T(8,128)(2,1)}, bf16[32,768]{1,0:T(8,128)(2,1)}, u32[]{:S(2)}, u32[]{:S(2)}) %collective-permute-start.13) | collective-permute-done | bytes 49184 | tf_op jit(solution)/shard_map/ppermute | solution.py:65
  159.1 7.4 %shard_map.113.so_far = f32[512,768]{1,0:T(8,128)} custom-call(s32[2,896]{1,0:T(2,128)} %bitcast.34, s32[32]{0:T(128)} %sel.5, s32[36]{0:T(128)} %get-tuple-element.25.index, bf16[8,3,32,128]{3,2,1,0:T(8,128)(2,1)} %copy-done.3, bf16[28,32,128]{2,1,0:T(8,128)(2,1)} %get-tuple-element.29.rows, bf16[8,32,768]{2,1,0:T(8,128)(2,1)} %get-tuple-element.42.near_grads, ...), custom_call_target="tpu_custom_call" | custom-call | flops 352321536 | bytes 924944 | tf_op jit(solution)/shard_map/pallas_call | solution.py:80
  170.1 3.9 %shard_map.115.refs_0_ = f32[768,768]{1,0:T(8,128)} custom-call(f32[256,768]{1,0:T(8,128)} %bitcast.28, f32[256,768]{1,0:T(8,128)} %get-tuple-element.41.pre_grad.refs_1_), custom_call_target="tpu_custom_call" | custom-call | flops 905969664 | bytes 1572864 | tf_op jit(solution)/shard_map/pallas_call | solution.py:80
  174.0 3.1 %shard_map.114 = f32[512,768]{1,0:T(8,128)} custom-call(s32[36]{0:T(128)} %get-tuple-element.25.index, f32[512,768]{1,0:T(8,128)} %shard_map.113.so_far, bf16[2,32,128]{2,1,0:T(8,128)(2,1)} %copy-done.17, bf16[2,32,128]{2,1,0:T(8,128)(2,1)} %copy-done.18, bf16[2,32,128]{2,1,0:T(8,128)(2,1)} %copy-done.19, ...), custom_call_target="tpu_custom_call", output_to_operand_aliasing={{}: (1, {})} | custom-call | flops 352321536 | bytes 1769616 | tf_op jit(solution)/shard_map/pallas_call | solution.py:80
  177.8 1.8 shard_map.120
  180.5 4.6 %shard_map.116.refs_0_ = f32[768,768]{1,0:T(8,128)} custom-call(f32[768,768]{1,0:T(8,128)} %shard_map.115.refs_0_, f32[256,768]{1,0:T(8,128)} %collective-permute-done.16.refs_1_, f32[256,768]{1,0:T(8,128)} %copy-done.10), custom_call_target="tpu_custom_call", output_to_operand_aliasing={{}: (0, {})} | custom-call | flops 905969664 | bytes 3932160 | tf_op jit(solution)/shard_map/pallas_call | solution.py:80
  185.1 4.6 %shard_map.117.refs_0_ = f32[768,768]{1,0:T(8,128)} custom-call(f32[768,768]{1,0:T(8,128)} %shard_map.116.refs_0_, f32[256,768]{1,0:T(8,128)} %copy-done.9, f32[256,768]{1,0:T(8,128)} %copy-done.8), custom_call_target="tpu_custom_call", output_to_operand_aliasing={{}: (0, {})} | custom-call | flops 905969664 | bytes 3932160 | tf_op jit(solution)/shard_map/pallas_call | solution.py:80
  189.7 4.6 %shard_map.118 = f32[768,768]{1,0:T(8,128)} custom-call(f32[768,768]{1,0:T(8,128)} %shard_map.117.refs_0_, f32[256,768]{1,0:T(8,128)} %collective-permute-done.20.refs_1_, f32[256,768]{1,0:T(8,128)} %collective-permute-done.21.refs_2_), custom_call_target="tpu_custom_call", output_to_operand_aliasing={{}: (0, {})} | custom-call | flops 905969664 | bytes 3932160 | tf_op jit(solution)/shard_map/pallas_call | solution.py:80
  (114 shorter events, 21.6 us)
Async XLA Ops:
  4.0 18.6 %all-to-all-start = ((bf16[8,3,32,128]{3,2,1,0:T(8,128)(2,1)}), bf16[8,3,32,128]{3,2,1,0:T(8,128)(2,1)S(1)}, u32[]{:S(2)}, u32[]{:S(2)}) async-start(bf16[8,3,32,128]{3,2,1,0:T(8,128)(2,1)} %get-tuple-element.26), calls=%async_computation | async-start | bytes 393216 | tf_op jit(solution)/shard_map/all_to_all | solution.py:413
  11.3 21.1 %collective-permute-start.6 = (f32[32,768]{1,0:T(8,128)}, f32[32,768]{1,0:T(8,128)S(1)}, u32[]{:S(2)}, u32[]{:S(2)}) collective-permute-start(f32[32,768]{1,0:T(8,128)} %texts.1), channel_id=1, source_target_pairs={{2,0},{3,1},{4,2},{5,3},{6,4},{7,5},{0,6},{1,7},{10,8},{11,9},{12,... | collective-permute-start | bytes 294920 | tf_op jit(solution)/shard_map/ppermute | solution.py:65
  15.1 18.1 %collective-permute-start.7 = (f32[32,768]{1,0:T(8,128)}, f32[32,768]{1,0:T(8,128)S(1)}, u32[]{:S(2)}, u32[]{:S(2)}) collective-permute-start(f32[32,768]{1,0:T(8,128)} %texts.1), channel_id=1, source_target_pairs={{4,0},{5,1},{6,2},{7,3},{0,4},{1,5},{2,6},{3,7},{12,8},{13,9},{14,... | collective-permute-start | bytes 294920 | tf_op jit(solution)/shard_map/ppermute | solution.py:65
  15.1 18.1 %collective-permute-start.8 = (f32[32,768]{1,0:T(8,128)}, f32[32,768]{1,0:T(8,128)S(1)}, u32[]{:S(2)}, u32[]{:S(2)}) collective-permute-start(f32[32,768]{1,0:T(8,128)} %texts.1), channel_id=1, source_target_pairs={{6,0},{7,1},{0,2},{1,3},{2,4},{3,5},{4,6},{5,7},{14,8},{15,9},{8,1... | collective-permute-start | bytes 294920 | tf_op jit(solution)/shard_map/ppermute | solution.py:65
  26.0 46.0 %all-to-all-start.1 = ((f32[8,32,768]{2,1,0:T(8,128)}), f32[8,32,768]{2,1,0:T(8,128)S(1)}, u32[]{:S(2)}, u32[]{:S(2)}) async-start(f32[8,32,768]{2,1,0:T(8,128)} %shard_map.104), calls=%async_computation.1 | async-start | bytes 1572864 | tf_op jit(solution)/shard_map/all_to_all | solution.py:432
  30.9 4.4 %collective-permute-start = (bf16[2,32,128]{2,1,0:T(8,128)(2,1)S(1)}, bf16[2,32,128]{2,1,0:T(8,128)(2,1)S(1)}, u32[]{:S(2)}, u32[]{:S(2)}) collective-permute-start(bf16[2,32,128]{2,1,0:T(8,128)(2,1)S(1)} %get-tuple-element.51), channel_id=1, source_target_pairs={{16,0},{24,8},{0,16},{8,24},{17,1},{25,9},{1,17},{9,25},{18,2},{26... | collective-permute-start | bytes 49160 | tf_op jit(solution)/shard_map/ppermute | solution.py:65
  32.4 2.9 %collective-permute-start.1 = (bf16[2,32,128]{2,1,0:T(8,128)(2,1)S(1)}, bf16[2,32,128]{2,1,0:T(8,128)(2,1)S(1)}, u32[]{:S(2)}, u32[]{:S(2)}) collective-permute-start(bf16[2,32,128]{2,1,0:T(8,128)(2,1)S(1)} %get-tuple-element.53), channel_id=1, source_target_pairs={{8,0},{0,8},{24,16},{16,24},{9,1},{1,9},{25,17},{17,25},{10,2},{2,... | collective-permute-start | bytes 49160 | tf_op jit(solution)/shard_map/ppermute | solution.py:65
  32.5 3.2 %collective-permute-start.2 = (bf16[2,32,128]{2,1,0:T(8,128)(2,1)S(1)}, bf16[2,32,128]{2,1,0:T(8,128)(2,1)S(1)}, u32[]{:S(2)}, u32[]{:S(2)}) collective-permute-start(bf16[2,32,128]{2,1,0:T(8,128)(2,1)S(1)} %get-tuple-element.52), channel_id=1, source_target_pairs={{24,0},{16,8},{8,16},{0,24},{25,1},{17,9},{9,17},{1,25},{26,2},{18... | collective-permute-start | bytes 49160 | tf_op jit(solution)/shard_map/ppermute | solution.py:65
  33.2 16.5 %collective-permute-start.9 = (f32[128,768]{1,0:T(8,128)S(1)}, f32[128,768]{1,0:T(8,128)S(1)}, u32[]{:S(2)}, u32[]{:S(2)}) collective-permute-start(f32[128,768]{1,0:T(8,128)S(1)} %pad_maximum_fusion), channel_id=1, source_target_pairs={{1,0},{0,1},{3,2},{2,3},{5,4},{4,5},{7,6},{6,7},{9,8},{8,9},{11,10... | collective-permute-start | bytes 1179656 | tf_op jit(solution)/shard_map/ppermute | solution.py:65
  35.3 16.1 %copy-start.17 = (bf16[2,32,128]{2,1,0:T(8,128)(2,1)}, bf16[2,32,128]{2,1,0:T(8,128)(2,1)S(1)}, u32[]{:S(2)}) copy-start(bf16[2,32,128]{2,1,0:T(8,128)(2,1)S(1)} %collective-permute-done.refs_0_) | copy-start | bytes 49156
  35.3 16.1 %copy-start.18 = (bf16[2,32,128]{2,1,0:T(8,128)(2,1)}, bf16[2,32,128]{2,1,0:T(8,128)(2,1)S(1)}, u32[]{:S(2)}) copy-start(bf16[2,32,128]{2,1,0:T(8,128)(2,1)S(1)} %collective-permute-done.1.refs_1_) | copy-start | bytes 49156
  35.7 15.7 %copy-start.19 = (bf16[2,32,128]{2,1,0:T(8,128)(2,1)}, bf16[2,32,128]{2,1,0:T(8,128)(2,1)S(1)}, u32[]{:S(2)}) copy-start(bf16[2,32,128]{2,1,0:T(8,128)(2,1)S(1)} %collective-permute-done.2.refs_2_) | copy-start | bytes 49156
  49.8 31.0 %copy-start.6 = (f32[256,768]{1,0:T(8,128)}, f32[256,768]{1,0:T(8,128)S(1)}, u32[]{:S(2)}) copy-start(f32[256,768]{1,0:T(8,128)S(1)} %constant_dynamic-update-slice_fusion.refs_0_) | copy-start | bytes 2359300
  49.8 31.5 %collective-permute-start.10 = (f32[256,768]{1,0:T(8,128)S(1)}, f32[256,768]{1,0:T(8,128)S(1)}, u32[]{:S(2)}, u32[]{:S(2)}) collective-permute-start(f32[256,768]{1,0:T(8,128)S(1)} %constant_dynamic-update-slice_fusion.refs_0_), channel_id=1, source_target_pairs={{16,0},{24,8},{0,16},{8,24},{17,1},{25,9},{1,17},{9,25},{18,2},{26... | collective-permute-start | bytes 2359304 | tf_op jit(solution)/shard_map/ppermute | solution.py:65
  51.5 20.4 %collective-permute-start.3 = (f32[32,768]{1,0:T(8,128)S(1)}, f32[32,768]{1,0:T(8,128)S(1)}, u32[]{:S(2)}, u32[]{:S(2)}) collective-permute-start(f32[32,768]{1,0:T(8,128)S(1)} %get-tuple-element.48), channel_id=1, source_target_pairs={{16,0},{24,8},{0,16},{8,24},{17,1},{25,9},{1,17},{9,25},{18,2},{26... | collective-permute-start | bytes 294920 | tf_op jit(solution)/shard_map/ppermute | solution.py:65
  52.0 19.9 %collective-permute-start.4 = (f32[32,768]{1,0:T(8,128)S(1)}, f32[32,768]{1,0:T(8,128)S(1)}, u32[]{:S(2)}, u32[]{:S(2)}) collective-permute-start(f32[32,768]{1,0:T(8,128)S(1)} %get-tuple-element.47), channel_id=1, source_target_pairs={{8,0},{0,8},{24,16},{16,24},{9,1},{1,9},{25,17},{17,25},{10,2},{2,... | collective-permute-start | bytes 294920 | tf_op jit(solution)/shard_map/ppermute | solution.py:65
  52.0 20.0 %collective-permute-start.5 = (f32[32,768]{1,0:T(8,128)S(1)}, f32[32,768]{1,0:T(8,128)S(1)}, u32[]{:S(2)}, u32[]{:S(2)}) collective-permute-start(f32[32,768]{1,0:T(8,128)S(1)} %get-tuple-element.46), channel_id=1, source_target_pairs={{24,0},{16,8},{8,16},{0,24},{25,1},{17,9},{9,17},{1,25},{26,2},{18... | collective-permute-start | bytes 294920 | tf_op jit(solution)/shard_map/ppermute | solution.py:65
  75.7 25.9 %all-to-all-start.2 = ((f32[8,32,768]{2,1,0:T(8,128)}), f32[8,32,768]{2,1,0:T(8,128)S(1)}, u32[]{:S(2)}, u32[]{:S(2)}) async-start(f32[8,32,768]{2,1,0:T(8,128)} %shard_map.107), calls=%async_computation.2 | async-start | bytes 1572864 | tf_op jit(solution)/shard_map/all_to_all | solution.py:477
  80.8 6.3 %collective-permute-start.11 = (f32[256,768]{1,0:T(8,128)S(1)}, f32[256,768]{1,0:T(8,128)S(1)}, u32[]{:S(2)}, u32[]{:S(2)}) collective-permute-start(f32[256,768]{1,0:T(8,128)S(1)} %constant_dynamic-update-slice_fusion.refs_0_), channel_id=1, source_target_pairs={{8,0},{0,8},{24,16},{16,24},{9,1},{1,9},{25,17},{17,25},{10,2},{2,... | collective-permute-start | bytes 2359304 | tf_op jit(solution)/shard_map/ppermute | solution.py:65
  81.3 5.8 %collective-permute-start.12 = (f32[256,768]{1,0:T(8,128)S(1)}, f32[256,768]{1,0:T(8,128)}, u32[]{:S(2)}, u32[]{:S(2)}) collective-permute-start(f32[256,768]{1,0:T(8,128)S(1)} %collective-permute-done.10.refs_1_), channel_id=1, source_target_pairs={{8,0},{0,8},{24,16},{16,24},{9,1},{1,9},{25,17},{17,25},{10,2},{2,... | collective-permute-start | bytes 2359304 | tf_op jit(solution)/shard_map/ppermute | solution.py:65
  121.8 36.7 %collective-permute-start.19 = (f32[256,768]{1,0:T(8,128)}, f32[256,768]{1,0:T(8,128)S(1)}, u32[]{:S(2)}, u32[]{:S(2)}) collective-permute-start(f32[256,768]{1,0:T(8,128)} %get-tuple-element.41.pre_grad.refs_1_), channel_id=1, source_target_pairs={{16,0},{24,8},{0,16},{8,24},{17,1},{25,9},{1,17},{9,25},{18,2},{26... | collective-permute-start | bytes 2359304 | tf_op jit(solution)/shard_map/ppermute | solution.py:65
  122.8 36.3 %collective-permute-start.18 = (f32[256,768]{1,0:T(8,128)S(1)}, f32[256,768]{1,0:T(8,128)S(1)}, u32[]{:S(2)}, u32[]{:S(2)}) collective-permute-start(f32[256,768]{1,0:T(8,128)S(1)} %bitcast.29), channel_id=1, source_target_pairs={{16,0},{24,8},{0,16},{8,24},{17,1},{25,9},{1,17},{9,25},{18,2},{26... | collective-permute-start | bytes 2359304 | tf_op jit(solution)/shard_map/ppermute | solution.py:65
  127.8 30.7 %collective-permute-start.13 = (bf16[32,768]{1,0:T(8,128)(2,1)}, bf16[32,768]{1,0:T(8,128)(2,1)}, u32[]{:S(2)}, u32[]{:S(2)}) collective-permute-start(bf16[32,768]{1,0:T(8,128)(2,1)} %get-tuple-element.44), channel_id=1, source_target_pairs={{16,0},{24,8},{0,16},{8,24},{17,1},{25,9},{1,17},{9,25},{18,2},{26... | collective-permute-start | bytes 147464 | tf_op jit(solution)/shard_map/ppermute | solution.py:65
  128.8 50.8 %collective-permute-start.17 = (f32[256,768]{1,0:T(8,128)}, f32[256,768]{1,0:T(8,128)S(1)}, u32[]{:S(2)}, u32[]{:S(2)}) collective-permute-start(f32[256,768]{1,0:T(8,128)} %get-tuple-element.41.pre_grad.refs_1_), channel_id=1, source_target_pairs={{8,0},{0,8},{24,16},{16,24},{9,1},{1,9},{25,17},{17,25},{10,2},{2,... | collective-permute-start | bytes 2359304 | tf_op jit(solution)/shard_map/ppermute | solution.py:65
  128.8 50.8 %collective-permute-start.16 = (f32[256,768]{1,0:T(8,128)S(1)}, f32[256,768]{1,0:T(8,128)}, u32[]{:S(2)}, u32[]{:S(2)}) collective-permute-start(f32[256,768]{1,0:T(8,128)S(1)} %bitcast.30), channel_id=1, source_target_pairs={{8,0},{0,8},{24,16},{16,24},{9,1},{1,9},{25,17},{17,25},{10,2},{2,... | collective-permute-start | bytes 2359304 | tf_op jit(solution)/shard_map/ppermute | solution.py:65
  132.3 34.7 %copy-start.4 = (f32[4,32,768]{2,1,0:T(8,128)S(1)}, f32[4,32,768]{2,1,0:T(8,128)}, u32[]{:S(2)}) copy-start(f32[4,32,768]{2,1,0:T(8,128)} %shard_map.119) | copy-start | bytes 1179652
  158.5 8.0 %collective-permute-start.22 = (f32[2,32,768]{2,1,0:T(8,128)}, f32[2,32,768]{2,1,0:T(8,128)}, u32[]{:S(2)}, u32[]{:S(2)}) collective-permute-start(f32[2,32,768]{2,1,0:T(8,128)} %slice.61), channel_id=1, source_target_pairs={{8,0},{0,8},{24,16},{16,24},{9,1},{1,9},{25,17},{17,25},{10,2},{2,... | collective-permute-start | bytes 589832 | tf_op jit(solution)/shard_map/ppermute | solution.py:65
  158.5 31.2 %collective-permute-start.21 = (f32[256,768]{1,0:T(8,128)S(1)}, f32[256,768]{1,0:T(8,128)}, u32[]{:S(2)}, u32[]{:S(2)}) collective-permute-start(f32[256,768]{1,0:T(8,128)S(1)} %collective-permute-done.19.refs_2_), channel_id=1, source_target_pairs={{8,0},{0,8},{24,16},{16,24},{9,1},{1,9},{25,17},{17,25},{10,2},{2,... | collective-permute-start | bytes 2359304 | tf_op jit(solution)/shard_map/ppermute | solution.py:65
  159.0 30.6 %collective-permute-start.20 = (f32[256,768]{1,0:T(8,128)S(1)}, f32[256,768]{1,0:T(8,128)}, u32[]{:S(2)}, u32[]{:S(2)}) collective-permute-start(f32[256,768]{1,0:T(8,128)S(1)} %collective-permute-done.18.refs_1_), channel_id=1, source_target_pairs={{8,0},{0,8},{24,16},{16,24},{9,1},{1,9},{25,17},{17,25},{10,2},{2,... | collective-permute-start | bytes 2359304 | tf_op jit(solution)/shard_map/ppermute | solution.py:65
  166.6 1.6 collective-permute-start.14
  168.1 1.4 collective-permute-start.15
  169.6 7.5 %collective-permute-start.23 = (f32[32,768]{1,0:T(8,128)S(1)}, f32[32,768]{1,0:T(8,128)S(1)}, u32[]{:S(2)}, u32[]{:S(2)}) collective-permute-start(f32[32,768]{1,0:T(8,128)S(1)} %get-tuple-element.49), channel_id=1, source_target_pairs={{16,0},{24,8},{0,16},{8,24},{17,1},{25,9},{1,17},{9,25},{18,2},{26... | collective-permute-start | bytes 294920 | tf_op jit(solution)/shard_map/ppermute | solution.py:65
  (18 other events, 75.2 us)
